TPU v7x, 32 devices: a whole 2x2x4 slice. The times are simulated.
32 devices in a mesh: emb: 32 (over z, y, x, core).
Axes of the slice: x: 2, y: 2, z: 4, core: 2. Of those that a mesh axis runs over, the one named last changes fastest.
Arguments:
- tok_ids: int32 [32768], P('emb')
- x_in: bfloat16 [32768, 1024], P('emb')
- d_out: bfloat16 [32768, 1024], P('emb')
- ple_tables: bfloat16 [3, 151936, 256], P(None, 'emb')
- w_up: bfloat16 [3, 1024, 3072], replicated
- w_down: bfloat16 [3, 3072, 1024], replicated
- w_gate: bfloat16 [3, 1024, 256], replicated
- w_proj: bfloat16 [3, 256, 1024], replicated
Outputs:
- output 1: bfloat16 [32768, 1024], P('emb')
- output 2: float32 [3, 151936, 256], P(None, 'emb')
- output 3: float32 [3, 1024, 3072], replicated
- output 4: float32 [3, 3072, 1024], replicated
- output 5: float32 [3, 1024, 256], replicated
- output 6: float32 [3, 256, 1024], replicated
All inputs are finite; a program needn't handle non-finite values.
Results may differ from a plain program's by a relative error of at most 0.0144084.
Values are sent between devices in bfloat16 or wider.
A program may use at most 1 GiB of HBM per device.

v0:
```python
import jax
import jax.numpy as jnp
from jax import lax
from jax.sharding import PartitionSpec as P

EPS = 1e-6
CAP_DIV = 4


def gelu_tanh(pre_act):
    return jax.nn.gelu(pre_act, approximate=True)


def gelu_back(pre_act, grad_out):
    _, pull_back = jax.vjp(gelu_tanh, pre_act.astype(jnp.float32))
    return pull_back(grad_out.astype(jnp.float32))[0]


def layer_fwd(x_cur, up_mat, down_mat, gate_mat, proj_mat, emb_rows):
    x_wide = x_cur.astype(jnp.float32)
    inv_rms = lax.rsqrt(jnp.mean(x_wide * x_wide, axis=-1, keepdims=True) + EPS)
    normed = (x_wide * inv_rms).astype(jnp.bfloat16)
    hidden = jnp.dot(normed, up_mat, preferred_element_type=jnp.float32).astype(jnp.bfloat16)
    act_out = gelu_tanh(hidden.astype(jnp.float32)).astype(jnp.bfloat16)
    mlp_out = jnp.dot(act_out, down_mat, preferred_element_type=jnp.float32).astype(jnp.bfloat16)
    gate_pre = jnp.dot(normed, gate_mat, preferred_element_type=jnp.float32).astype(jnp.bfloat16)
    gate_act = gelu_tanh(gate_pre.astype(jnp.float32)).astype(jnp.bfloat16)
    mix_rows = (gate_act.astype(jnp.float32) * emb_rows.astype(jnp.float32)).astype(jnp.bfloat16)
    ple_out = jnp.dot(mix_rows, proj_mat, preferred_element_type=jnp.float32).astype(jnp.bfloat16)
    x_next = (x_wide + mlp_out.astype(jnp.float32) + ple_out.astype(jnp.float32)).astype(jnp.bfloat16)
    return x_next, (x_wide, inv_rms, normed, hidden, act_out, gate_pre, gate_act, mix_rows)


def layer_bwd(d_x, saved, emb_rows, up_mat, down_mat, gate_mat, proj_mat):
    x_wide, inv_rms, normed, hidden, act_out, gate_pre, gate_act, mix_rows = saved
    g_out = d_x.astype(jnp.bfloat16)
    d_act = jnp.einsum("nd,fd->nf", g_out, down_mat, preferred_element_type=jnp.float32).astype(jnp.bfloat16)
    d_hidden = gelu_back(hidden, d_act).astype(jnp.bfloat16)
    d_mix = jnp.einsum("nd,ed->ne", g_out, proj_mat, preferred_element_type=jnp.float32).astype(jnp.bfloat16)
    d_rows = gate_act.astype(jnp.float32) * d_mix.astype(jnp.float32)
    d_gate_act = (emb_rows.astype(jnp.float32) * d_mix.astype(jnp.float32)).astype(jnp.bfloat16)
    d_gate_pre = gelu_back(gate_pre, d_gate_act).astype(jnp.bfloat16)
    d_norm = jnp.einsum("nf,df->nd", d_hidden, up_mat, preferred_element_type=jnp.float32) + jnp.einsum("ne,de->nd", d_gate_pre, gate_mat, preferred_element_type=jnp.float32)
    d_x_new = d_x + inv_rms * d_norm - inv_rms ** 3 * x_wide * jnp.mean(d_norm * x_wide, axis=-1, keepdims=True)
    g_up = jnp.einsum("nd,nf->df", normed, d_hidden, preferred_element_type=jnp.float32)
    g_down = jnp.einsum("nf,nd->fd", act_out, g_out, preferred_element_type=jnp.float32)
    g_gate = jnp.einsum("nd,ne->de", normed, d_gate_pre, preferred_element_type=jnp.float32)
    g_proj = jnp.einsum("ne,nd->ed", mix_rows, g_out, preferred_element_type=jnp.float32)
    return d_x_new, (g_up, g_down, g_gate, g_proj), d_rows


def solution(mesh):
    shards = mesh.shape["emb"]

    def device_step(tok_ids, x_in, d_out, ple_tables, w_up, w_down, w_gate, w_proj):
        layers = ple_tables.shape[0]
        rows_dev = ple_tables.shape[1]
        cap_rows = tok_ids.shape[0] // CAP_DIV
        owner_dev = tok_ids // rows_dev
        local_row = tok_ids - owner_dev * rows_dev
        owner_hot = (owner_dev[:, None] == jnp.arange(shards, dtype=jnp.int32)[None, :]).astype(jnp.int32)
        slot_rank = jnp.sum((jnp.cumsum(owner_hot, axis=0) - owner_hot) * owner_hot, axis=1)
        dest_slot = owner_dev * cap_rows + slot_rank
        req_send = jnp.zeros((shards * cap_rows,), jnp.int32).at[dest_slot].set(local_row)
        req_recv = lax.all_to_all(req_send, "emb", 0, 0, tiled=True)
        x_cur = x_in
        saved_list = []
        rows_list = []
        for layer_idx in range(layers):
            served = jnp.take(ple_tables[layer_idx], req_recv, axis=0)
            returned = lax.all_to_all(served, "emb", 0, 0, tiled=True)
            emb_rows = jnp.take(returned, dest_slot, axis=0)
            x_cur, saved = layer_fwd(x_cur, w_up[layer_idx], w_down[layer_idx], w_gate[layer_idx], w_proj[layer_idx], emb_rows)
            saved_list.append(saved)
            rows_list.append(emb_rows)
        d_x = d_out.astype(jnp.float32)
        grads_by_layer = [None] * layers
        tables_by_layer = [None] * layers
        for layer_idx in reversed(range(layers)):
            d_x, grads, d_rows = layer_bwd(d_x, saved_list[layer_idx], rows_list[layer_idx], w_up[layer_idx], w_down[layer_idx], w_gate[layer_idx], w_proj[layer_idx])
            grad_send = jnp.zeros((shards * cap_rows, d_rows.shape[1]), jnp.float32).at[dest_slot].set(d_rows)
            grad_recv = lax.all_to_all(grad_send, "emb", 0, 0, tiled=True)
            tables_by_layer[layer_idx] = jax.ops.segment_sum(grad_recv, req_recv, num_segments=rows_dev)
            grads_by_layer[layer_idx] = lax.psum(grads, "emb")
        grad_stacks = [jnp.stack([entry[grad_pos] for entry in grads_by_layer]) for grad_pos in range(4)]
        return (x_cur, jnp.stack(tables_by_layer), grad_stacks[0], grad_stacks[1], grad_stacks[2], grad_stacks[3])

    return jax.shard_map(
        device_step,
        mesh=mesh,
        in_specs=(P("emb"), P("emb", None), P("emb", None), P(None, "emb", None), P(), P(), P(), P()),
        out_specs=(P("emb", None), P(None, "emb", None), P(), P(), P(), P()),
        check_vma=False,
    )
```

profile of v0, /device:TPU:0, one launch (start us, length us, event | category | flops | bytes accessed | tf_op | source)
XLA Modules:
  0.0 2315.3 jit_solution(5134124737757687385)
XLA Ops:
  37.5 33.2 %gather_fusion = bf16[8192,256]{1,0:T(8,128)(2,1)} fusion(bf16[4748,256]{1,0:T(8,128)(2,1)} %get-tuple-element.41, s32[8192]{0:T(1024)S(1)} %fusion.223), kind=kCustom, calls=%fused_computation.clone | custom fusion | bytes 8421376 | tf_op jit(solution)/shard_map/jit(_take)/gather | solution.py:70
  70.7 33.2 %gather_fusion.2 = bf16[8192,256]{1,0:T(8,128)(2,1)} fusion(bf16[4748,256]{1,0:T(8,128)(2,1)} %get-tuple-element.42, s32[8192]{0:T(1024)S(1)} %fusion.223), kind=kCustom, calls=%fused_computation.2.clone | custom fusion | bytes 8421376 | tf_op jit(solution)/shard_map/jit(_take)/gather | solution.py:70
  103.8 33.2 %gather_fusion.4 = bf16[8192,256]{1,0:T(8,128)(2,1)} fusion(bf16[4748,256]{1,0:T(8,128)(2,1)S(1)} %get-tuple-element.40, s32[8192]{0:T(1024)S(1)} %fusion.223), kind=kCustom, calls=%fused_computation.3.clone | custom fusion | bytes 8421376 | tf_op jit(solution)/shard_map/jit(_take)/gather | solution.py:70
  145.3 99.4 %all_to_all.84 = bf16[32,256,256]{2,1,0:T(8,128)(2,1)} all-to-all(bf16[32,256,256]{2,1,0:T(8,128)(2,1)S(1)} %bitcast.176), channel_id=1, replica_groups=mesh['emb'=32] {'emb'}, dimensions={0} | all-to-all | bytes 8388608 | tf_op jit(solution)/shard_map/all_to_all | solution.py:71
  261.3 11.7 fusion.61
  282.7 12.5 fusion.89
  297.8 11.7 fusion.64
  309.5 33.4 %all-to-all-done.2 = bf16[32,256,256]{2,1,0:T(8,128)(2,1)} async-done(((bf16[32,256,256]{2,1,0:T(8,128)(2,1)}), bf16[32,256,256]{2,1,0:T(8,128)(2,1)}, u32[]{:S(2)}, u32[]{:S(2)}) %all-to-all-start.2) | async-done | bytes 4194336 | tf_op jit(solution)/shard_map/all_to_all | solution.py:71
  357.0 11.9 fusion.97
  381.4 19.5 fusion.5
  400.8 12.0 fusion.37
  412.8 28.4 %all-to-all-done.3 = bf16[32,256,256]{2,1,0:T(8,128)(2,1)} async-done(((bf16[32,256,256]{2,1,0:T(8,128)(2,1)}), bf16[32,256,256]{2,1,0:T(8,128)(2,1)}, u32[]{:S(2)}, u32[]{:S(2)}) %all-to-all-start.3) | async-done | bytes 4194336 | tf_op jit(solution)/shard_map/all_to_all | solution.py:71
  457.9 19.6 fusion.8
  479.8 12.3 convolution_bitcast_fusion.4
  492.1 10.8 fusion.45
  503.0 12.4 convolution_bitcast_fusion.3
  515.3 14.8 convolution_bitcast_fusion.1
  562.3 14.2 convolution_bitcast_fusion.2
  576.5 11.1 convolution_bitcast_fusion
  587.6 21.1 convolution_bitcast_fusion.5
  618.8 174.9 %all-to-all-done.4 = f32[32,256,256]{2,1,0:T(8,128)} async-done(((f32[32,256,256]{2,1,0:T(8,128)}), f32[32,256,256]{2,1,0:T(8,128)}, u32[]{:S(2)}, u32[]{:S(2)}) %all-to-all-start.4) | async-done | bytes 8388640 | tf_op jit(solution)/shard_map/all_to_all | solution.py:82
  793.8 23.8 %all-to-all-start.5 = ((f32[32,256,256]{2,1,0:T(8,128)}), f32[32,256,256]{2,1,0:T(8,128)}, u32[]{:S(2)}, u32[]{:S(2)}) async-start(f32[32,256,256]{2,1,0:T(8,128)} %bitcast.169), calls=%async_computation.5 | async-start | bytes 16777216 | tf_op jit(solution)/shard_map/all_to_all | solution.py:82
  826.8 263.6 %all-to-all-done.5 = f32[32,256,256]{2,1,0:T(8,128)} async-done(((f32[32,256,256]{2,1,0:T(8,128)}), f32[32,256,256]{2,1,0:T(8,128)}, u32[]{:S(2)}, u32[]{:S(2)}) %all-to-all-start.5) | async-done | bytes 8388640 | tf_op jit(solution)/shard_map/all_to_all | solution.py:82
  1096.4 12.3 fusion.100
  1112.7 58.1 %scatter_custom_fusion.2 = f32[4748,256]{1,0:T(8,128)} fusion(s32[8192]{0:T(1024)} %bitcast.186, f32[8192,256]{1,0:T(8,128)} %bitcast.27, f32[]{:T(128)} %constant.31.clone.1), kind=kCustom, calls=%fused_computation.156 | custom fusion | flops 2097152 | bytes 4862464 | tf_op jit(solution)/shard_map/scatter-add | solution.py:83
  1170.8 57.9 %scatter_custom_fusion.4 = f32[4748,256]{1,0:T(8,128)} fusion(s32[8192]{0:T(1024)} %bitcast.187, f32[8192,256]{1,0:T(8,128)} %bitcast.30, f32[]{:T(128)} %constant.31.clone.1), kind=kCustom, calls=%fused_computation.154 | custom fusion | flops 2097152 | bytes 4862464 | tf_op jit(solution)/shard_map/scatter-add | solution.py:83
  1228.6 138.7 %all-to-all-done.6 = f32[32,256,256]{2,1,0:T(8,128)} async-done(((f32[32,256,256]{2,1,0:T(8,128)}), f32[32,256,256]{2,1,0:T(8,128)}, u32[]{:S(2)}, u32[]{:S(2)}) %all-to-all-start.6) | async-done | bytes 8388640 | tf_op jit(solution)/shard_map/all_to_all | solution.py:82
  1367.3 57.8 %scatter_custom_fusion.6 = f32[4748,256]{1,0:T(8,128)} fusion(s32[8192]{0:T(1024)} %bitcast.188, f32[8192,256]{1,0:T(8,128)} %bitcast.33, f32[]{:T(128)} %constant.31.clone.1), kind=kCustom, calls=%fused_computation.152 | custom fusion | flops 2097152 | bytes 4862464 | tf_op jit(solution)/shard_map/scatter-add | solution.py:83
  1425.1 11.9 pad_maximum_fusion.2
  1437.1 816.5 %all-reduce.3.cloned.1.call-done = (f32[1,1024,3072]{2,1,0:T(8,128)}, f32[1,1024,3072]{2,1,0:T(8,128)}, f32[1,1024,3072]{2,1,0:T(8,128)}, f32[1,3072,1024]{2,1,0...) async-done(((f32[1,1024,3072]{2,1,0:T(8,128)}, ...) | async-done | bytes 81788944 | tf_op jit(solution)/shard_map/psum | solution.py:84
  2259.6 32.4 %pad_maximum_fusion.1 = f32[3,3072,1024]{2,1,0:T(8,128)} fusion(f32[1,3072,1024]{2,1,0:T(8,128)} %get-tuple-element.29, f32[1,3072,1024]{2,1,0:T(8,128)} %get-tuple-element.30, f32[1,3072,1024]{2,1,0:T(8,128)} %get-tuple-element.31), kind=kLoop, calls=%fused_computation.14 | loop fusion | flops 18874368 | bytes 75497472 | tf_op jit(solution)/shard_map/stack | solution.py:85
  2295.5 12.5 pad_maximum_fusion
  (162 shorter events, 183.4 us)
Async XLA Ops:
  18.1 236.4 %copy-start.33 = (s32[1024]{0:T(1024)}, s32[1024]{0:T(1024)S(1)}, u32[]{:S(2)}) copy-start(s32[1024]{0:T(1024)S(1)} %get-tuple-element.39) | copy-start | bytes 12292
  23.0 14.5 all-to-all-start
  37.5 33.2 %copy-start.31 = (s32[32,256,1]{1,2,0:T(1,128)}, s32[32,256,1]{1,2,0:T(1,128)S(1)}, u32[]{:S(2)}) copy-start(s32[32,256,1]{1,2,0:T(1,128)S(1)} %all-to-all-done) | copy-start | bytes 98308
  244.8 98.1 %all-to-all-start.2 = ((bf16[32,256,256]{2,1,0:T(8,128)(2,1)}), bf16[32,256,256]{2,1,0:T(8,128)(2,1)}, u32[]{:S(2)}, u32[]{:S(2)}) async-start(bf16[32,256,256]{2,1,0:T(8,128)(2,1)} %bitcast.175), calls=%async_computation.2 | async-start | bytes 8388608 | tf_op jit(solution)/shard_map/all_to_all | solution.py:71
  259.2 193.7 %copy-start.10 = (bf16[1024,256]{1,0:T(8,128)(2,1)}, bf16[1024,256]{1,0:T(8,128)(2,1)S(1)}, u32[]{:S(2)}) copy-start(bf16[1024,256]{1,0:T(8,128)(2,1)S(1)} %convolution_convert_fusion.2) | copy-start | bytes 1572868
  261.3 19.1 copy-start.27
  297.8 56.9 %copy-start.12 = (bf16[1024,256]{1,0:T(8,128)(2,1)}, bf16[1024,256]{1,0:T(8,128)(2,1)S(1)}, u32[]{:S(2)}) copy-start(bf16[1024,256]{1,0:T(8,128)(2,1)S(1)} %fusion.143) | copy-start | bytes 1572868
  342.9 98.3 %all-to-all-start.3 = ((bf16[32,256,256]{2,1,0:T(8,128)(2,1)}), bf16[32,256,256]{2,1,0:T(8,128)(2,1)}, u32[]{:S(2)}, u32[]{:S(2)}) async-start(bf16[32,256,256]{2,1,0:T(8,128)(2,1)} %bitcast.174), calls=%async_computation.3 | async-start | bytes 8388608 | tf_op jit(solution)/shard_map/all_to_all | solution.py:71
  369.0 12.4 copy-start
  381.4 19.5 copy-start.36
  457.8 76.9 %copy-start.14 = (bf16[1024,256]{1,0:T(8,128)(2,1)}, bf16[1024,256]{1,0:T(8,128)(2,1)S(1)}, u32[]{:S(2)}) copy-start(bf16[1024,256]{1,0:T(8,128)(2,1)S(1)} %convolution_convert_fusion.1) | copy-start | bytes 1572868
  457.9 19.7 copy-start.13
  457.9 19.7 copy-start.22
  515.3 14.8 copy-start.18
  554.4 239.3 %all-to-all-start.4 = ((f32[32,256,256]{2,1,0:T(8,128)}), f32[32,256,256]{2,1,0:T(8,128)}, u32[]{:S(2)}, u32[]{:S(2)}) async-start(f32[32,256,256]{2,1,0:T(8,128)} %bitcast.167), calls=%async_computation.4 | async-start | bytes 16777216 | tf_op jit(solution)/shard_map/all_to_all | solution.py:82
  558.8 1694.8 %all-reduce.3.cloned.1.call-start = ((), (), s32[]{:S(2)}) async-start(), calls=%async_computation.7 | async-start | bytes 163577856 | tf_op jit(solution)/shard_map/psum | solution.py:84
  558.8 17.7 slice-start.9
  562.3 14.2 copy-start.19
  562.3 14.2 slice-start.10
  576.5 11.1 copy-start.5
  793.8 23.8 %copy-start.11 = (bf16[1024,256]{1,0:T(8,128)(2,1)S(1)}, bf16[1024,256]{1,0:T(8,128)(2,1)}, u32[]{:S(2)}) copy-start(bf16[1024,256]{1,0:T(8,128)(2,1)} %copy-done.10) | copy-start | bytes 1572868
  793.8 296.6 %all-to-all-start.5 = ((f32[32,256,256]{2,1,0:T(8,128)}), f32[32,256,256]{2,1,0:T(8,128)}, u32[]{:S(2)}, u32[]{:S(2)}) async-start(f32[32,256,256]{2,1,0:T(8,128)} %bitcast.169), calls=%async_computation.5 | async-start | bytes 16777216 | tf_op jit(solution)/shard_map/all_to_all | solution.py:82
  1090.4 276.9 %all-to-all-start.6 = ((f32[32,256,256]{2,1,0:T(8,128)}), f32[32,256,256]{2,1,0:T(8,128)}, u32[]{:S(2)}, u32[]{:S(2)}) async-start(f32[32,256,256]{2,1,0:T(8,128)} %bitcast.168), calls=%async_computation.6 | async-start | bytes 16777216 | tf_op jit(solution)/shard_map/all_to_all | solution.py:82
  2259.5 32.5 %slice-start = ((s8[12582912]{0:T(1024)(128)(4,1)}), s8[4194304]{0:T(1024)(128)(4,1)S(1)}, s32[]{:S(2)}) async-start(s8[12582912]{0:T(1024)(128)(4,1)} %bitcast.177), calls=%async_computation.8 | async-start | bytes 8388608
  2259.5 32.5 %slice-start.3 = ((s8[12582912]{0:T(1024)(128)(4,1)}), s8[4194304]{0:T(1024)(128)(4,1)S(1)}, s32[]{:S(2)}) async-start(s8[12582912]{0:T(1024)(128)(4,1)} %bitcast.179), calls=%async_computation.11 | async-start | bytes 8388608
  2259.5 32.5 %slice-start.6 = ((s8[12582912]{0:T(1024)(128)(4,1)}), s8[4194304]{0:T(1024)(128)(4,1)S(1)}, s32[]{:S(2)}) async-start(s8[12582912]{0:T(1024)(128)(4,1)} %bitcast.181), calls=%async_computation.14 | async-start | bytes 8388608
  2259.5 32.5 %slice-start.1 = ((s8[12582912]{0:T(1024)(128)(4,1)}), s8[4194304]{0:T(1024)(128)(4,1)S(1)}, s32[]{:S(2)}) async-start(s8[12582912]{0:T(1024)(128)(4,1)} %bitcast.177), calls=%async_computation.9 | async-start | bytes 8388608
  2259.5 32.5 %slice-start.2 = ((s8[12582912]{0:T(1024)(128)(4,1)}), s8[4194304]{0:T(1024)(128)(4,1)S(1)}, s32[]{:S(2)}) async-start(s8[12582912]{0:T(1024)(128)(4,1)} %bitcast.177), calls=%async_computation.10 | async-start | bytes 8388608
  2259.5 32.5 %slice-start.4 = ((s8[12582912]{0:T(1024)(128)(4,1)}), s8[4194304]{0:T(1024)(128)(4,1)S(1)}, s32[]{:S(2)}) async-start(s8[12582912]{0:T(1024)(128)(4,1)} %bitcast.179), calls=%async_computation.12 | async-start | bytes 8388608
  2259.5 33.6 %slice-start.5 = ((s8[12582912]{0:T(1024)(128)(4,1)}), s8[4194304]{0:T(1024)(128)(4,1)S(1)}, s32[]{:S(2)}) async-start(s8[12582912]{0:T(1024)(128)(4,1)} %bitcast.179), calls=%async_computation.13 | async-start | bytes 8388608
  2259.5 34.8 %slice-start.7 = ((s8[12582912]{0:T(1024)(128)(4,1)}), s8[4194304]{0:T(1024)(128)(4,1)S(1)}, s32[]{:S(2)}) async-start(s8[12582912]{0:T(1024)(128)(4,1)} %bitcast.181), calls=%async_computation.15 | async-start | bytes 8388608
  2259.6 36.0 %slice-start.8 = ((s8[12582912]{0:T(1024)(128)(4,1)}), s8[4194304]{0:T(1024)(128)(4,1)S(1)}, s32[]{:S(2)}) async-start(s8[12582912]{0:T(1024)(128)(4,1)} %bitcast.181), calls=%async_computation.16 | async-start | bytes 8388608
  (23 other events, 102.4 us)
Sparse Core Ops, SparseCore 0:
  608.9 1644.6 all-reduce.2
where the time goes:
time: 2320 us
  waiting for transfers between devices  1460 us (63%)
  other arithmetic  291 us (13%)
  matrix products  258 us (11%)
  local copies, waits for them, and re-layouts  147 us (6%)
  blocking collectives  99.4 us (4%)
  starting transfers between devices  48.2 us (2%)
    psum x1, waiting for transfers between devices, device_step(): grads_by_layer[layer_idx] = lax.psum(grads, 'emb')  816 us
    all_to_all x3, waiting for transfers between devices, device_step(): grad_recv = lax.all_to_all(grad_send, 'emb', 0, 0, tiled=True)  577 us
    scatter-add x3, other arithmetic, device_step(): jax.ops.segment_sum(grad_recv, req_recv, num_segments=rows_dev)  174 us
    gather x3, local copies, waits for them, and re-layouts, device_step(): served = jnp.take(ple_tables[layer_idx], req_recv, axis=0)  99.5 us
    all_to_all x1, blocking collectives, device_step(): returned = lax.all_to_all(served, 'emb', 0, 0, tiled=True)  99.4 us
    all_to_all x2, waiting for transfers between devices, device_step(): returned = lax.all_to_all(served, 'emb', 0, 0, tiled=True)  61.7 us
    another operation x4, other arithmetic, device_step(): jnp.stack([entry[grad_pos] for entry in grads_by_layer])  50.9 us
  transfers between devices with their start and end apart: 7, of which 7 were waited for; matrix products, arithmetic and copies ran while one was open for 17% of the time, Pallas kernels for 0%

commit v1 on v0

v1 whole, which is shorter than its diff:
```python
import functools

import jax
import jax.numpy as jnp
from jax import lax
from jax.experimental import pallas as pl
from jax.experimental.layout import Layout, with_layout_constraint
from jax.experimental.pallas import tpu as pltpu
from jax.sharding import PartitionSpec as P


EPS = 1e-6
CAP_DIV = 4


def gelu_tanh(pre_act):
    return jax.nn.gelu(pre_act, approximate=True)


def gelu_back(pre_act, grad_out):
    _, pull_back = jax.vjp(gelu_tanh, pre_act.astype(jnp.float32))
    return pull_back(grad_out.astype(jnp.float32))[0]


def dot32(a, b, dims):
    return lax.dot_general(a, b, (dims, ((), ())), preferred_element_type=jnp.float32)


def layer_fwd(x_cur, up_mat, down_mat, gate_mat, proj_mat, emb_rows):
    x_wide = x_cur.astype(jnp.float32)
    inv_rms = lax.rsqrt(jnp.mean(x_wide * x_wide, **ROW) + EPS)
    normed = (x_wide * inv_rms).astype(jnp.bfloat16)
    hidden = jnp.dot(normed, up_mat, preferred_element_type=jnp.float32).astype(jnp.bfloat16)
    act_out = gelu_tanh(hidden.astype(jnp.float32)).astype(jnp.bfloat16)
    mlp_out = jnp.dot(act_out, down_mat, preferred_element_type=jnp.float32).astype(jnp.bfloat16)
    gate_pre = jnp.dot(normed, gate_mat, preferred_element_type=jnp.float32).astype(jnp.bfloat16)
    gate_act = gelu_tanh(gate_pre.astype(jnp.float32)).astype(jnp.bfloat16)
    mix_rows = (gate_act.astype(jnp.float32) * emb_rows.astype(jnp.float32)).astype(jnp.bfloat16)
    ple_out = jnp.dot(mix_rows, proj_mat, preferred_element_type=jnp.float32).astype(jnp.bfloat16)
    x_next = (x_wide + mlp_out.astype(jnp.float32) + ple_out.astype(jnp.float32)).astype(jnp.bfloat16)
    return x_next, (x_cur, inv_rms, normed, hidden, act_out, gate_pre, gate_act, mix_rows)


def layer_bwd(d_x, saved, emb_rows, up_mat, down_mat, gate_mat, proj_mat, last):
    x_cur, inv_rms, normed, hidden, act_out, gate_pre, gate_act, mix_rows = saved
    x_wide = x_cur.astype(jnp.float32)
    g_out = d_x.astype(jnp.bfloat16)
    d_act = dot32(g_out, down_mat, NT).astype(jnp.bfloat16)
    d_hidden = gelu_back(hidden, d_act).astype(jnp.bfloat16)
    d_mix = dot32(g_out, proj_mat, NT).astype(jnp.bfloat16)
    d_gate_act = (emb_rows.astype(jnp.float32) * d_mix.astype(jnp.float32)).astype(jnp.bfloat16)
    d_gate_pre = gelu_back(gate_pre, d_gate_act).astype(jnp.bfloat16)
    d_x_new = None
    if not last:
        d_norm = dot32(d_hidden, up_mat, NT) + dot32(d_gate_pre, gate_mat, NT)
        d_x_new = d_x + inv_rms * d_norm - inv_rms ** 3 * x_wide * jnp.mean(d_norm * x_wide, **ROW)
    return d_x_new, (normed, act_out, mix_rows, g_out, d_hidden, d_gate_pre), (gate_act, d_mix)


AXES = ("far", "near", "y", "x", "core")
WEIGHT = {name: 1 << i for i, name in enumerate(reversed(AXES))}
ORDERS = (("core", "x", "y", "near", "far"), ("core", "y", "near", "x", "far"), ("core", "near", "x", "y", "far"))
MESH = pl.DeviceIdType.MESH
DEPTH = 2
FIRST = range(DEPTH)
LAG = 2
NN, NT, TN = ((1,), (0,)), ((1,), (1,)), ((0,), (0,))
ROW = {"axis": -1, "keepdims": True}
HALF, QUART, EIGHTH = 128, 64, 32


def bit(v):
    return lax.rem(v, 2)


def loop(first, last, body):
    def step(i, carry):
        body(i)
        return carry

    lax.fori_loop(first, last, step, 0)


def swap(a):
    return lax.all_to_all(a, "emb", 0, 0, tiled=True)


def line(i):
    return pl.ds(i, 1)


def col(v):
    return v[:, None]


def row(v):
    return v[None, :]


def numbers(n):
    return jnp.arange(n, dtype=jnp.int32)


BLK = 256
NB = 16
NS = 8


def reduce_kernel(sizes, *refs):
    n_layers, per, n = sizes
    u_0, a_0, us, as_, ss, os_, dhs, dzs, send_t, out, tails = refs[:11]
    (v_as, v_o, v_u, v_d, blk1, blk2, blk3, rc1, rc2, rc3, rf1, rf2, rs1, rs2, ri1, ri2, rm1, rm2, fin1, fin2,
     ri3, rm3, rx3, rf3, rs3, fin3, ssem, rsem, lsem, osem, tv, tsem, trsem, tlsem) = refs[11:]
    me = lax.axis_index("emb")
    core, x, y, z = bit(me), bit(me // 2), bit(me // 4), me // 8
    mid = (z == 1) | (z == 2)
    end = (z == 0) | (z == 3)
    zb = z // 2
    p_core = me + 1 - 2 * core
    p_x = me + 2 - 4 * x
    p_y = me + 4 - 8 * y
    step_in = jnp.where((z == 0) | (z == 1), 8, -8)
    p_side = jnp.where((z == 0) | (z == 2), me + 8, me - 8)
    p_mid = jnp.where(z == 1, me + 8, jnp.where(z == 2, me - 8, me))

    barrier = pltpu.get_barrier_semaphore()
    p_far = me + 16 - EIGHTH * zb
    for dev in (p_core, p_x, p_y, p_side, p_far):
        pl.semaphore_signal(barrier, inc=1, device_id=(dev,), device_id_type=MESH)

    @pl.when(mid)
    def _():
        pl.semaphore_signal(barrier, inc=1, device_id=(p_mid,), device_id_type=MESH)
        pl.semaphore_wait(barrier, 6)

    @pl.when(end)
    def _():
        pl.semaphore_wait(barrier, 5)

    def loads(ell):
        layer = n_layers - 1 - ell
        u, a = (us.at[layer - 1], as_.at[layer - 1]) if layer else (u_0, a_0)
        s, o, dh, dz = (t.at[layer] for t in (ss, os_, dhs, dzs))
        slot = ell % 2
        hid = a_0.shape[1]
        left, right = pl.ds(0, hid), pl.ds(hid, BLK)
        ways = ((a, v_as.at[slot, :, left]), (s, v_as.at[slot, :, right]), (o, v_o.at[slot]), (u, v_u.at[slot]),
                (dh, v_d.at[slot, :, left]), (dz, v_d.at[slot, :, right]))
        return [pltpu.make_async_copy(src, dst, osem.at[slot, i]) for i, (src, dst) in enumerate(ways)]

    emb = tv.shape[2]
    spot = {"far": z // 2, "near": bit(z), "y": y, "x": x, "core": core}
    other = {"far": p_far, "near": p_side, "y": p_y, "x": p_x, "core": p_core}
    t_half = tv.shape[1] // 2

    def tail_copy(layer, s, p):
        order = tuple(reversed(ORDERS[layer]))
        block = p // 2
        at = {name: bit(block // (1 << t)) for t, name in enumerate(order[:s])}
        where = tuple(at.get(name, spot[name]) for name in AXES)
        ref = tails.at[(layer,) + where + (pl.ds(pl.multiple_of(bit(p) * t_half, t_half), t_half),)]
        i = lax.rem(p, 4)
        return pltpu.make_async_remote_copy(src_ref=ref, dst_ref=ref, send_sem=tsem.at[layer, s, i], recv_sem=trsem.at[layer, s, i],
                                            device_id=(other[order[s]],), device_id_type=MESH)

    t_first = [4]
    for s in range(len(AXES)):
        t_first.append(t_first[-1] + (2 << s) + 2)
    t_in = [pltpu.make_async_copy(send_t.at[:, pl.ds(k * emb, emb)], tv.at[k], tlsem.at[k]) for k in range(n_layers)]
    t_own = [pltpu.make_async_copy(tv.at[k], tails.at[(k,) + tuple(spot[name] for name in AXES)], tlsem.at[k]) for k in range(n_layers)]
    for c in t_in:
        c.start()
    for c, d in zip(t_in, t_own):
        c.wait()
        d.start()
    for c in t_own:
        c.wait()
    for ell in (0, 1):
        for c in loads(ell):
            c.start()
    for c in loads(0):
        c.wait()

    span = n // n_layers
    rest = {0: 2, 1: 4}

    def active(k, kind):
        return True if kind == 2 else lax.rem(k, 5) != rest[kind]

    def unit(k, kind):
        t = lax.rem(k, span)
        if kind == 2:
            return span * 4 // 5 + t // 2
        p = lax.rem(t, 5)
        return 4 * (t // 5) + p - (p > rest[kind]).astype(jnp.int32)

    def where_out(k, kind):
        base = {0: 0, 1: per, 2: per * bit(k)}[kind]
        return (n_layers - 1 - k // span) * 2 * per + base + unit(k, kind)

    def block(slot, w, wide):
        if wide:
            rb, cb = w // 13, lax.rem(w, 13)
            lhs, rhs = v_u, v_d
        else:
            rb, cb = lax.rem(w, 13), w // 13
            lhs, rhs = v_as, v_o
        lv = lhs[slot, :, pl.ds(pl.multiple_of(rb * BLK, BLK), BLK)]
        rv = rhs[slot, :, pl.ds(pl.multiple_of(cb * BLK, BLK), BLK)]
        return dot32(lv, rv, TN)

    h0 = core * HALF
    flows = []

    def add_flow(off, src, dst, dev, send_if=None, recv_if=None):
        flows.append((len(flows), off, src, dst, dev, send_if, recv_if))
        return flows[-1]

    def rows(start, size):
        return pl.ds(pl.multiple_of(start, EIGHTH), size)

    def desc(f, k):
        idx, _, src, dst, dev, _, _ = f
        d = dev(k) if callable(dev) else dev
        return pltpu.make_async_remote_copy(
            src_ref=src(k), dst_ref=dst(k), send_sem=ssem.at[idx, lax.rem(k, NB)], recv_sem=rsem.at[idx, lax.rem(k, NB)],
            device_id=(d,), device_id_type=MESH)

    def ok(k, cond):
        v = (k >= 0) & (k < n)
        return v if cond is None else v & (cond(k) if callable(cond) else cond)

    acts = []

    def clock():
        now = [-1]

        def at(more=LAG):
            now[0] += more
            return now[0]

        return at

    def xyz(kind, blk, rc, rf, rs, ri, rm, fin, f, s, p_f, p_s):
        at = clock()
        q0, q1 = h0 + f * QUART, h0 + (1 - f) * QUART
        e0, e1 = q0 + s * EIGHTH, q0 + (1 - s) * EIGHTH
        b = lambda k: lax.rem(k, NB)
        m = lambda k: lax.rem(k, NS)
        o = lambda k: where_out(k, kind)
        go = lambda k: active(k, kind)
        on = lambda side: (lambda k: side & active(k, kind))
        f_core = add_flow(at(), lambda k: blk.at[b(k), rows(HALF - h0, HALF)], lambda k: rc.at[m(k)], p_core, go, go)
        f_first = add_flow(at(), lambda k: blk.at[b(k), rows(q1, QUART)], lambda k: rf.at[m(k)], p_f, go, go)
        f_second = add_flow(at(), lambda k: blk.at[b(k), rows(e1, EIGHTH)], lambda k: rs.at[m(k)], p_s, go, go)
        f_in = add_flow(at(), lambda k: blk.at[b(k), rows(e0, EIGHTH)], lambda k: ri.at[m(k)], p_side, on(end), on(mid))
        f_mid = add_flow(at(), lambda k: blk.at[b(k), rows(e0, EIGHTH)], lambda k: rm.at[m(k)], p_mid, on(mid), on(mid))
        f_out = add_flow(at(), lambda k: fin.at[b(k)], lambda k: fin.at[b(k)], p_side, on(mid), on(end))
        g_s = add_flow(at(), lambda k: fin.at[b(k)], lambda k: out.at[o(k), rows(e0, EIGHTH)], p_s, go, go)
        g_f = add_flow(at(), lambda k: out.at[o(k), rows(q0, QUART)], lambda k: out.at[o(k), rows(q0, QUART)], p_f, go, go)
        g_c = add_flow(at(), lambda k: out.at[o(k), rows(h0, HALF)], lambda k: out.at[o(k), rows(h0, HALF)], p_core, go, go)

        def plus(dst0, size, src):
            def add(k):
                r = rows(dst0, size)
                blk[b(k), r] = blk[b(k), r] + src[m(k)]

            return add

        def final(k):
            fin[b(k)] = blk[b(k), rows(e0, EIGHTH)] + rm[m(k)]

        acts.append((f_core, plus(h0, HALF, rc)))
        acts.append((f_first, plus(q0, QUART, rf)))
        acts.append((f_second, plus(e0, EIGHTH, rs)))
        acts.append((f_in, plus(e0, EIGHTH, ri)))
        acts.append((f_mid, final))
        acts.extend((g, None) for g in (f_out, g_s, g_f, g_c))
        locals_.append((g_s[1], lambda k: pltpu.make_async_copy(fin.at[b(k)], out.at[o(k), rows(e0, EIGHTH)], lsem.at[kind, m(k)]), go))

    def zfirst(kind, blk, rc, ri, rm, rx, rf, rs, fin):
        at = clock()
        odd = lambda k: bit(k) == 1
        at_end = lambda k: bit(k // 2) == 1
        here = lambda k: jnp.where(at_end(k), end, mid)
        q0, q1 = h0 + zb * QUART, h0 + (1 - zb) * QUART
        b = lambda k: lax.rem(k, NB)
        m = lambda k: lax.rem(k, NS)
        o = lambda k: where_out(k, kind)
        f = lambda k: jnp.where(odd(k), y, x)
        e0 = lambda k: q0 + f(k) * EIGHTH
        e1 = lambda k: q0 + (1 - f(k)) * EIGHTH
        p_f = lambda k: jnp.where(odd(k), p_y, p_x)
        p_s = lambda k: jnp.where(odd(k), p_x, p_y)
        e_root = lambda side: (lambda k: side & at_end(k))
        m_root = lambda side: (lambda k: side & jnp.logical_not(at_end(k)))
        f_core = add_flow(at(), lambda k: blk.at[b(k), rows(HALF - h0, HALF)], lambda k: rc.at[m(k)], p_core)
        f_in = add_flow(at(), lambda k: blk.at[b(k), rows(h0, HALF)], lambda k: ri.at[b(k)], p_side, m_root(end), m_root(mid))
        f_in2 = add_flow(at(0), lambda k: blk.at[b(k), rows(q1, QUART)], lambda k: ri.at[b(k), pl.ds(0, QUART)], p_side, e_root(end), e_root(mid))
        f_mid = add_flow(at(), lambda k: blk.at[b(k), rows(q1, QUART)], lambda k: rm.at[m(k)], p_mid, mid, mid)
        f_x = add_flow(at(), lambda k: blk.at[b(k), rows(q0, QUART)], lambda k: rx.at[m(k)], p_side, e_root(mid), e_root(end))
        f_first = add_flow(at(), lambda k: blk.at[b(k), rows(e1(k), EIGHTH)], lambda k: rf.at[m(k)], p_f, here, here)
        f_second = add_flow(at(), lambda k: blk.at[b(k), rows(e0(k), EIGHTH)], lambda k: rs.at[m(k)], p_s, here, here)
        g_f = add_flow(at(), lambda k: fin.at[m(k)], lambda k: out.at[o(k), rows(e0(k), EIGHTH)], p_f, here, here)
        g_x = add_flow(at(), lambda k: out.at[o(k), rows(q0, QUART)], lambda k: out.at[o(k), rows(q0, QUART)], p_side, e_root(end), e_root(mid))
        g_m = add_flow(at(), lambda k: out.at[o(k), rows(q0, QUART)], lambda k: out.at[o(k), rows(q0, QUART)], p_mid, mid, mid)
        g_o = add_flow(at(), lambda k: out.at[o(k), rows(h0, HALF)], lambda k: out.at[o(k), rows(h0, HALF)], p_side, m_root(mid), m_root(end))
        g_o2 = add_flow(at(0), lambda k: out.at[o(k), rows(q1, QUART)], lambda k: out.at[o(k), rows(q1, QUART)], p_side, e_root(mid), e_root(end))
        g_c = add_flow(at(), lambda k: out.at[o(k), rows(h0, HALF)], lambda k: out.at[o(k), rows(h0, HALF)], p_core)

        def plus(start, size, src):
            def go(k):
                r = rows(start(k), size)
                blk[b(k), r] = blk[b(k), r] + src(k)

            return go

        def final(k):
            fin[m(k)] = blk[b(k), rows(e0(k), EIGHTH)] + rs[m(k)]

        acts.append((f_core, plus(lambda k: h0, HALF, lambda k: rc[m(k)])))
        acts.append((f_in, plus(lambda k: h0, HALF, lambda k: ri[b(k)])))
        acts.append((f_in2, plus(lambda k: q1, QUART, lambda k: ri[b(k), :QUART])))
        acts.append((f_mid, plus(lambda k: q0, QUART, lambda k: rm[m(k)])))
        acts.append((f_x, plus(lambda k: q0, QUART, lambda k: rx[m(k)])))
        acts.append((f_first, plus(e0, EIGHTH, lambda k: rf[m(k)])))
        acts.append((f_second, final))
        acts.extend((g, None) for g in (g_f, g_x, g_m, g_o, g_o2, g_c))
        locals_.append((g_f[1], lambda k: pltpu.make_async_copy(fin.at[m(k)], out.at[o(k), rows(e0(k), EIGHTH)], lsem.at[kind, m(k)]), here))

    locals_ = []
    xyz(0, blk1, rc1, rf1, rs1, ri1, rm1, fin1, x, y, p_x, p_y)
    xyz(1, blk2, rc2, rf2, rs2, ri2, rm2, fin2, y, x, p_y, p_x)
    zfirst(2, blk3, rc3, ri3, rm3, rx3, rf3, rs3, fin3)

    def round_(r):
        for f in flows:
            _, off, _, _, _, give, _ = f
            k = r - off - LAG - LAG

            @pl.when(ok(k, give))
            def _(f=f, k=k):
                desc(f, k).wait_send()
        for off, mk, cond in locals_:
            k = r - off - LAG

            @pl.when(ok(k, cond))
            def _(mk=mk, k=k):
                mk(k).wait()
        for f, fn in acts:
            _, off, _, _, _, _, take = f
            k = r - off - LAG

            @pl.when(ok(k, take))
            def _(f=f, fn=fn, k=k):
                desc(f, k).wait_recv()
                if fn is not None:
                    fn(k)
        for s in range(len(AXES)):
            p = r - t_first[s]

            @pl.when((p >= 2) & (p < (2 << s) + 2))
            def _(s=s, p=p):
                for k in range(n_layers):
                    tail_copy(k, s, p - 2).wait()

            @pl.when((p >= 0) & (p < (2 << s)))
            def _(s=s, p=p):
                for k in range(n_layers):
                    tail_copy(k, s, p).start()
        for ell in range(1, n_layers):
            @pl.when(r == span * ell)
            def _(ell=ell):
                for c in loads(ell):
                    c.wait()
        for f in flows:
            _, off, _, _, _, give, _ = f
            k = r - off

            @pl.when(ok(k, give))
            def _(f=f, k=k):
                desc(f, k).start()
        for off, mk, cond in locals_:
            k = r - off

            @pl.when(ok(k, cond))
            def _(mk=mk, k=k):
                mk(k).start()

        slot = bit(r // span)
        s = lax.rem(r, NB)
        odd = bit(r) == 1

        @pl.when((r < n) & active(r, 0))
        def _():
            blk1[s] = block(slot, unit(r, 0), False)

        @pl.when((r < n) & active(r, 1))
        def _():
            blk2[s] = block(slot, unit(r, 1), True)

        @pl.when((r < n) & odd)
        def _():
            blk3[s] = block(slot, unit(r, 2), True)

        @pl.when((r < n) & jnp.logical_not(odd))
        def _():
            blk3[s] = block(slot, unit(r, 2), False)

        for ell in range(2, n_layers):
            @pl.when(r == span * (ell - 1) - 1)
            def _(ell=ell):
                for c in loads(ell):
                    c.start()

    loop(0, n + 25, round_)


def reduce_grads(u_0, a_0, us, as_, ss, os_, dhs, dzs, send_t):
    n_layers, toks, wide = ss.shape[0], u_0.shape[0], a_0.shape[1] + ss.shape[2]
    dim = u_0.shape[1]
    over, emb = send_t.shape[0], ss.shape[2]
    per = (wide // BLK) * (dim // BLK)
    n = per * 10 // 13 * n_layers
    f32, bf = jnp.float32, jnp.bfloat16
    V = pltpu.VMEM

    def many(count, slots, rows):
        return [V((slots, rows, BLK), f32)] * count

    big, small = (DEPTH, toks, wide), (DEPTH, toks, dim)
    scratch = [V(big, bf), V(small, bf), V(small, bf), V(big, bf)]
    scratch += many(3, NB, BLK) + many(3, NS, HALF) + many(DEPTH, NS, QUART) + many(6, NS, EIGHTH) + many(DEPTH, NB, EIGHTH)
    scratch += many(1, NB, HALF) + many(DEPTH, NS, QUART) + many(3, NS, EIGHTH)
    D = pltpu.SemaphoreType.DMA
    scratch += [D((31, NB)), D((31, NB)), D((3, NS)), D((DEPTH, 6))]
    scratch += [V((n_layers, over, emb), f32)] + [D((n_layers, len(AXES), LAG + LAG))] * DEPTH + [D((n_layers,))]
    flat = (u_0, a_0, us, as_, ss, os_, dhs, dzs, send_t)
    return pl.pallas_call(
        functools.partial(reduce_kernel, (n_layers, per, n)),
        out_shape=[jax.ShapeDtypeStruct((2 * per * n_layers, BLK, BLK), f32),
                   jax.ShapeDtypeStruct((n_layers,) + (2,) * len(AXES) + (over, emb), f32)],
        in_specs=[pl.BlockSpec(memory_space=pl.ANY)] * len(flat),
        out_specs=[pl.BlockSpec(memory_space=pl.ANY)] * 2,
        scratch_shapes=scratch,
        compiler_params=pltpu.CompilerParams(collective_id=0, has_side_effects=True, vmem_limit_bytes=66_000_000),
        cost_estimate=pl.CostEstimate(flops=600 * 10**9, bytes_accessed=10**8, transcendentals=0),
        name="reduce_grads",
    )(*flat)


TILE = 256
FCH = 512
GK = 0.7978845608028654
GC = 0.044715


def gelu_f(h):
    return (0.5 * h) * (1.0 + jnp.tanh(h * (GK + (GK * GC) * (h * h))))


def gelu_g(h, g):
    h2 = h * h
    t = jnp.tanh(h * (GK + (GK * GC) * h2))
    return g * (0.5 * (1.0 + t) + (0.5 * h) * (1.0 - t * t) * (GK + (3.0 * GK * GC) * h2))


def model_kernel(*refs):
    (x0, m0, h0, z0, g0, base, t0, t1, t2, pick, pick_t, d_out, w_up, w_down, w_gate, w_proj,
     x_out, us, as_, ss, os_, dhs, dzs, hs, send_b, send_t,
     wug, wd, wp, wp0, xs, cs, hbuf, abuf, ubuf, obuf, pbuf, sbuf, zs, es, gs, invs, dus, dsv, sb, st,
     wsem, usem, hsem, asem, osem, isem, jsem, psem, ssem, zsem, vsem) = refs
    f32, bf = jnp.float32, jnp.bfloat16
    slots = base.shape[0]
    n_tiles = xs.shape[1] // TILE
    top = es.shape[0] - 1
    ends = range(n_tiles - DEPTH, n_tiles)
    hid = hbuf.shape[2]
    emb = wp0.shape[0]
    dim = wp0.shape[1]

    def rows(i):
        return pl.ds(pl.multiple_of(i * TILE, TILE), TILE)

    def mm(a, b):
        return dot32(a, b, NN)

    def mt(a, b):
        return dot32(a, b, NT)

    cp = pltpu.make_async_copy

    def weights(layer, slot):
        ways = ((w_up, wug.at[slot, :, pl.ds(0, hid)]), (w_down, wd.at[slot]), (w_gate, wug.at[slot, :, pl.ds(hid, emb)]), (w_proj, wp.at[slot]))
        return [cp(src.at[layer], dst, wsem.at[slot, i]) for i, (src, dst) in enumerate(ways)]

    first = cp(w_proj.at[0], wp0, wsem.at[0, 4])
    first.start()
    w1, w2 = weights(1, 0), weights(2, 1)
    for c in w1 + w2:
        c.start()

    def slot_of(i):
        return bit(i)

    def in_x(i):
        return cp(x0.at[rows(i)], ubuf.at[slot_of(i)], isem.at[slot_of(i)])

    def in_p(i):
        return cp(pick.at[rows(i)], pbuf.at[slot_of(i)], psem.at[slot_of(i)])

    def in_m(i):
        return cp(m0.at[rows(i)], obuf.at[slot_of(i)], jsem.at[slot_of(i)])

    def put(src, dst, layer, sem):
        return lambda i: cp(src.at[slot_of(i)], dst.at[layer, rows(i)] if layer is not None else dst.at[rows(i)], sem.at[slot_of(i)])

    tails = (t0, t1, t2)

    def rows_of(layer, i):
        in_p(i).wait()
        p = pbuf[slot_of(i)]
        return (mm(p[:, :slots], base[:, layer * emb:(layer + 1) * emb]) + mm(p[:, slots:], tails[layer][...])).astype(bf)

    for i in FIRST:
        in_x(i).start()
        in_m(i).start()
        in_p(i).start()
    first.wait()
    put_s = lambda layer: (lambda i: cp(sbuf.at[slot_of(i)], ss.at[layer, rows(i)], ssem.at[slot_of(i)]))

    def finish0(i):
        r, k = rows(i), slot_of(i)

        @pl.when(i >= DEPTH)
        def _():
            put_s(0)(i - DEPTH).wait()

        e = rows_of(0, i)
        es[0, r] = e
        s = (g0[r].astype(f32) * e.astype(f32)).astype(bf)
        sbuf[k] = s
        put_s(0)(i).start()
        q = mm(s, wp0[...]).astype(bf)
        in_x(i).wait()
        in_m(i).wait()
        xs[0, r] = (ubuf[k].astype(f32) + obuf[k].astype(f32) + q.astype(f32)).astype(bf)

        @pl.when(i + DEPTH < n_tiles)
        def _():
            in_x(i + DEPTH).start()
            in_m(i + DEPTH).start()
            in_p(i + DEPTH).start()

    loop(0, n_tiles, finish0)
    for i in ends:
        put_s(0)(i).wait()

    def fwd(layer, slot, loaded):
        below = layer - 1
        outs = [put(ubuf, us, below, usem), put(hbuf, hs, below, hsem), put_s(layer),
                lambda i: cp(abuf.at[slot_of(i), :, pl.ds(0, hid)], as_.at[below, rows(i)], asem.at[slot_of(i)])]
        if layer == top:
            outs.append(put(obuf, x_out, None, osem))
        for c in loaded:
            c.wait()
        for i in FIRST:
            in_p(i).start()

        def tile(i):
            r, k = rows(i), slot_of(i)

            @pl.when(i >= DEPTH)
            def _():
                for o in outs:
                    o(i - DEPTH).wait()

            x = xs[below, r].astype(f32)
            inv = lax.rsqrt(jnp.mean(x * x, **ROW) + EPS)
            invs[below, r] = jnp.broadcast_to(inv, (TILE, invs.shape[2]))
            u = (x * inv).astype(bf)
            ubuf[k] = u
            for c0 in range(0, hid, FCH):
                h = mm(u, wug[slot, :, c0:c0 + FCH]).astype(bf)
                hbuf[k, :, c0:c0 + FCH] = h
                abuf[k, :, c0:c0 + FCH] = gelu_f(h.astype(f32)).astype(bf)
            z = mm(u, wug[slot, :, hid:]).astype(bf)
            g = gelu_f(z.astype(f32)).astype(bf)
            zs[below, r] = z
            gs[below, r] = g
            e = rows_of(layer, i)
            es[layer, r] = e
            s = (g.astype(f32) * e.astype(f32)).astype(bf)
            sbuf[k] = s
            for c0 in range(0, dim, FCH):
                c1 = c0 + FCH
                q = mm(s, wp[slot, :, c0:c1]).astype(bf)
                m = mm(abuf[k, :, :hid], wd[slot, :, c0:c1]).astype(bf)
                new = (xs[below, r, c0:c1].astype(f32) + m.astype(f32) + q.astype(f32)).astype(bf)
                if layer == top:
                    obuf[k, :, c0:c1] = new
                else:
                    xs[layer, r, c0:c1] = new
            for o in outs:
                o(i).start()

            @pl.when(i + DEPTH < n_tiles)
            def _():
                in_p(i + DEPTH).start()

        loop(0, n_tiles, tile)
        for i in ends:
            for o in outs:
                o(i).wait()

    def in_h(layer, i):
        below = layer - 1
        return cp(h0.at[rows(i)] if layer == 0 else hs.at[below, rows(i)], hbuf.at[slot_of(i)], hsem.at[slot_of(i)])

    def bwd(layer, slot):
        below = layer - 1
        outs = [lambda i: cp(abuf.at[slot_of(i), :, pl.ds(0, hid)], dhs.at[layer, rows(i)], asem.at[slot_of(i)]),
                lambda i: cp(abuf.at[slot_of(i), :, pl.ds(hid, emb)], dzs.at[layer, rows(i)], zsem.at[slot_of(i)]),
                put(obuf, os_, layer, osem)]
        proj = wp0 if layer == 0 else wp.at[slot]

        def in_d(i):
            return cp(d_out.at[rows(i)], ubuf.at[slot_of(i)], isem.at[slot_of(i)])

        if layer == top:
            for i in FIRST:
                in_h(layer, i).start()
                in_d(i).start()

        def tile(i):
            r, k = rows(i), slot_of(i)

            @pl.when(i >= DEPTH)
            def _():
                for o in outs:
                    o(i - DEPTH).wait()

            if layer == top:
                in_d(i).wait()
                cs[r] = ubuf[k].astype(f32)
            o = cs[r].astype(bf)
            obuf[k] = o
            ds = mt(o, proj[...]).astype(bf)
            dsv[r] = ds
            z = (z0[r] if layer == 0 else zs[below, r]).astype(f32)
            dg = (es[layer, r].astype(f32) * ds.astype(f32)).astype(bf)
            abuf[k, :, hid:] = gelu_g(z, dg.astype(f32)).astype(bf)
            in_h(layer, i).wait()
            for c0 in range(0, hid, FCH):
                da = mt(o, wd[slot, c0:c0 + FCH]).astype(bf)
                abuf[k, :, c0:c0 + FCH] = gelu_g(hbuf[k, :, c0:c0 + FCH].astype(f32), da.astype(f32)).astype(bf)
            if layer > 0:
                dot = jnp.zeros((TILE, 1), f32)
                for c0 in range(0, dim, FCH):
                    du = mt(abuf[k], wug[slot, c0:c0 + FCH])
                    dus[:, c0:c0 + FCH] = du
                    dot = dot + jnp.sum(du * xs[below, r, c0:c0 + FCH].astype(f32), **ROW)
                inv = invs[below, r][:, :1]
                back = (inv * inv * inv) * (dot * (1.0 / dim))
                for c0 in range(0, dim, FCH):
                    c1 = c0 + FCH
                    cs[r, c0:c1] = cs[r, c0:c1] + inv * dus[:, c0:c1] - back * xs[below, r, c0:c1].astype(f32)
            for ot in outs:
                ot(i).start()

            @pl.when(i + DEPTH < n_tiles)
            def _():
                in_h(layer, i + DEPTH).start()
                if layer == top:
                    in_d(i + DEPTH).start()

        loop(0, n_tiles, tile)
        if layer > 0:
            for i in FIRST:
                in_h(below, i).start()
        g = g0 if layer == 0 else gs.at[below]
        d = g[...].astype(f32) * dsv[...].astype(f32)
        high = d.astype(bf)
        low = (d - high.astype(f32)).astype(bf)
        for c0 in range(0, slots, 256):
            p = pick_t[c0:c0 + 256]
            sb[c0:c0 + 256] = mm(p, high) + mm(p, low)
        p = pick_t[slots:]
        st[...] = mm(p, high) + mm(p, low)
        lanes = slice(layer * emb, (layer + 1) * emb)
        both = [cp(sb, send_b.at[:, lanes], vsem.at[0]), cp(st, send_t.at[:, lanes], vsem.at[1])]
        for c in both:
            c.start()
        for i in ends:
            for o in outs:
                o(i).wait()
        for c in both:
            c.wait()

    fwd(1, 0, w1)
    fwd(2, 1, w2)
    bwd(2, 1)
    last = cp(w_down.at[0], wd.at[1], wsem.at[1, 1])
    last.start()
    bwd(1, 0)
    last.wait()
    bwd(0, 1)


def run_model(pre, base, tails, pick, pick_t, d_out, w_up, w_down, w_gate, w_proj):
    x0, m0, h0, z0, g0 = pre
    layers, dim, hid = w_up.shape
    emb = w_gate.shape[2]
    toks = x0.shape[0]
    slots, over = base.shape[0], tails[0].shape[0]
    below = layers - 1
    f32, bf = jnp.float32, jnp.bfloat16
    hbm, vm = pl.BlockSpec(memory_space=pl.ANY), pl.BlockSpec(memory_space=pltpu.VMEM)
    S = jax.ShapeDtypeStruct
    V = pltpu.VMEM
    D = pltpu.SemaphoreType.DMA
    return pl.pallas_call(
        model_kernel,
        in_specs=[hbm] * 3 + [vm] * 6 + [hbm] + [vm] + [hbm] * 5,
        out_specs=[hbm] * 10,
        out_shape=[S((toks, dim), bf), S((below, toks, dim), bf), S((below, toks, hid), bf), S((layers, toks, emb), bf),
                   S((layers, toks, dim), bf), S((layers, toks, hid), bf), S((layers, toks, emb), bf), S((below, toks, hid), bf),
                   S((slots, layers * emb), f32), S((over, layers * emb), f32)],
        scratch_shapes=[
            V((DEPTH, dim, hid + emb), bf), V((DEPTH, hid, dim), bf), V((DEPTH, emb, dim), bf), V((emb, dim), bf),
            V((DEPTH, toks, dim), bf), V((toks, dim), f32), V((DEPTH, TILE, hid), bf), V((DEPTH, TILE, hid + emb), bf),
            V((DEPTH, TILE, dim), bf), V((DEPTH, TILE, dim), bf), V((DEPTH, TILE, slots + over), bf), V((DEPTH, TILE, emb), bf),
            V((DEPTH, toks, emb), bf), V((layers, toks, emb), bf), V((DEPTH, toks, emb), bf), V((DEPTH, toks, 128), f32), V((TILE, dim), f32),
            V((toks, emb), bf), V((slots, emb), f32), V((over, emb), f32),
            D((DEPTH, 5))] + [D((DEPTH,))] * 10,
        compiler_params=pltpu.CompilerParams(vmem_limit_bytes=67_000_000),
        name="model",
    )(x0, m0, h0, z0, g0, base, *tails, pick, pick_t, d_out, w_up, w_down, w_gate, w_proj)


BASE = 32
TAIL = 128


def spread(tok_ids, shards, rows_dev):
    toks = tok_ids.shape[0]
    i32, f32, bf = jnp.int32, jnp.float32, jnp.bfloat16
    owner = tok_ids // rows_dev
    local = tok_ids - owner * rows_dev
    row_no = lax.broadcasted_iota(i32, (toks, toks), 0)
    col_no = lax.broadcasted_iota(i32, (toks, toks), 1)
    same = col(tok_ids) == row(tok_ids)
    seen = jnp.max(jnp.where(same & (col_no < row_no), 1.0, 0.0), axis=1)
    new = 1.0 - seen
    hot32 = (col(owner) == row(numbers(shards))).astype(f32)
    fresh = hot32 * col(new)
    before = (row_no > col_no).astype(bf)
    ahead = jnp.dot(before, fresh.astype(bf), preferred_element_type=f32)
    rank = jnp.sum(ahead * hot32, axis=1)
    count = jnp.sum(fresh, axis=0)
    extra = jnp.maximum(count - BASE, 0.0)
    lower = lax.broadcasted_iota(i32, (shards, shards), 0) > lax.broadcasted_iota(i32, (shards, shards), 1)
    start = jnp.sum(jnp.where(lower, row(extra), 0.0), axis=1)
    tail = jnp.sum(hot32 * row(start), axis=1)
    place = jnp.where(rank < BASE, owner.astype(f32) * BASE + rank, shards * BASE + tail + rank - BASE)
    row_new = jnp.max(jnp.where(same & (row_no < col_no), 1.0, 0.0), axis=0) == 0.0
    slot = jnp.sum(jnp.where(same & row(row_new), row(place), 0.0), axis=1).astype(i32)
    n_slots = shards * BASE + TAIL
    pick = (col(slot) == lax.broadcasted_iota(i32, (toks, n_slots), 1)).astype(bf)
    pick_t = (row(slot) == lax.broadcasted_iota(i32, (n_slots, toks), 0)).astype(bf)
    parts = (jnp.stack([local // 64, local % 64], axis=1).astype(f32) * col(new)).astype(bf)
    want = jnp.dot(pick_t, parts, preferred_element_type=f32)
    want = (want[:, 0] * 64.0 + want[:, 1]).astype(i32)
    base = want[:shards * BASE].reshape(shards, BASE)
    rest = jnp.broadcast_to(want[shards * BASE:][None, :], (shards, TAIL))
    info = jnp.stack([count, start, extra, jnp.broadcast_to(jnp.sum(extra), (shards,))], axis=1).astype(i32)
    pad = jnp.zeros((shards, INFO - 4), i32)
    sent = jnp.concatenate([info, pad, base, rest], axis=1)
    got = swap(sent)
    return pick, pick_t, got


INFO = 128


def serve_kernel(n_layers, over, got, tables, *refs):
    base_out, outs, (tab, wide, stage, sem) = refs[0], refs[1:1 + n_layers], refs[1 + n_layers:]
    shards = got.shape[0]
    emb = wide.shape[2]
    loads = [pltpu.make_async_copy(tables.at[k], tab.at[k], sem.at[k]) for k in range(n_layers)]
    for c in loads:
        c.start()
    for k in range(n_layers):
        loads[k].wait()
        whole = wide.shape[1] // BLK * BLK

        def widen(i, k=k):
            r = pl.ds(pl.multiple_of(i * BLK, BLK), BLK)
            wide[k, r] = tab[k, r].astype(jnp.float32)

        loop(0, whole // BLK, widen)
        wide[k, whole:] = tab[k, whole:].astype(jnp.float32)

    def one(j):
        start, extra = got[j, 1], got[j, 2]

        def rows8(g):
            at = [got[j, INFO + g * 8 + i] for i in range(8)]
            for i in range(8):
                for k in range(n_layers):
                    stage[k, line(g * 8 + i)] = wide[k, line(at[i])]

        loop(0, BASE // 8, rows8)
        for k in range(n_layers):
            base_out[j, :, k * emb:(k + 1) * emb] = stage[k, :BASE].astype(jnp.bfloat16)

        @pl.when(extra == 0)
        def _():
            for k in range(n_layers):
                outs[k][j] = jnp.zeros((over, emb), jnp.bfloat16)

        @pl.when(extra > 0)
        def _():
            stage[...] = jnp.zeros_like(stage)

            def four(g):
                at = [got[j, INFO + BASE + start + g * 4 + i] for i in range(4)]
                for i in range(4):
                    for k in range(n_layers):
                        stage[k, line(start + g * 4 + i)] = wide[k, line(at[i])]

            def single(i):
                at = got[j, INFO + BASE + start + i]
                for k in range(n_layers):
                    stage[k, line(start + i)] = wide[k, line(at)]

            loop(0, extra // 4, four)
            loop(extra // 4 * 4, extra, single)
            for k in range(n_layers):
                outs[k][j] = stage[k].astype(jnp.bfloat16)

    loop(0, shards, one)


def serve(got, tables, over):
    n_layers, rows_dev, emb = tables.shape
    shards = got.shape[0]
    bf = jnp.bfloat16
    shapes = [jax.ShapeDtypeStruct((shards, BASE, n_layers * emb), bf)] + [jax.ShapeDtypeStruct((shards, over, emb), bf)] * n_layers
    return pl.pallas_call(
        functools.partial(serve_kernel, n_layers, over),
        in_specs=[pl.BlockSpec(memory_space=pltpu.SMEM), pl.BlockSpec(memory_space=pl.ANY)],
        out_specs=[pl.BlockSpec(memory_space=pltpu.VMEM)] * (1 + n_layers),
        out_shape=shapes,
        scratch_shapes=[pltpu.VMEM((n_layers, rows_dev, emb), bf), pltpu.VMEM((n_layers, rows_dev, emb), jnp.float32),
                        pltpu.VMEM((n_layers, over, emb), jnp.float32), pltpu.SemaphoreType.DMA((n_layers,))],
        compiler_params=pltpu.CompilerParams(vmem_limit_bytes=60_000_000),
        name="serve_rows",
    )(got, tables)


STEPS = 24


def finish_kernel(got, base, tail, total, table, down, proj, up, gate, base_v, tail_v, acc, sem):
    step = pl.program_id(0)
    shards = got.shape[0]
    n_layers, _, emb = acc.shape
    first = pltpu.make_async_copy(base, base_v, sem.at[0])
    second = pltpu.make_async_copy(tail, tail_v, sem.at[1])
    done = pltpu.make_async_copy(acc, table, sem.at[2])
    n = total.shape[0] - 1
    lanes = [slice(k * emb, (k + 1) * emb) for k in range(n_layers)]

    @pl.when(step == 0)
    def _():
        first.start()
        second.start()
        whole = acc.shape[1] // BLK * BLK
        for k in range(n_layers):
            def clear(i, k=k):
                acc[k, pl.ds(pl.multiple_of(i * BLK, BLK), BLK)] = jnp.zeros((BLK, emb), jnp.float32)

            loop(0, whole // BLK, clear)
            acc[k, whole:] = jnp.zeros((acc.shape[1] - whole, emb), jnp.float32)
        first.wait()

    @pl.when(step < STEPS // 2)
    def _():
        for c in range(n):
            down[0, c * BLK:(c + 1) * BLK] = total[c]
        proj[0] = total[n]

    @pl.when(step >= STEPS // 2)
    def _():
        for c in range(n):
            up[0, :, c * BLK:(c + 1) * BLK] = total[c]
        gate[0] = total[n]

    def one(j):
        def rows8(g):
            at = [line(got[j, INFO + g * 8 + i]) for i in range(8)]
            for i in range(8):
                for k in range(n_layers):
                    acc[k, at[i]] = acc[k, at[i]] + base_v[j, line(g * 8 + i), lanes[k]]

        loop(0, BASE // 8, rows8)

    def two(j):
        start, extra = got[j, 1], got[j, 2]

        def some(first_row, n):
            at = [line(got[j, INFO + BASE + start + first_row + i]) for i in range(n)]
            for i in range(n):
                for k in range(n_layers):
                    acc[k, at[i]] = acc[k, at[i]] + tail_v[k, j, line(start + first_row + i)]

        def four(g):
            some(g * 4, 4)

        def single(i):
            some(i, 1)

        loop(0, extra // 4, four)
        loop(extra // 4 * 4, extra, single)

    part = shards // 8

    @pl.when(step < 8)
    def _():
        loop(step * part, (step + 1) * part, one)

    @pl.when(step == 8)
    def _():
        second.wait()

    @pl.when((step >= 8) & (step < 16))
    def _():
        loop((step - 8) * part, (step - 7) * part, two)

    @pl.when(step == 17)
    def _():
        done.start()

    @pl.when(step == STEPS - 1)
    def _():
        done.wait()


def finish(got, base, tail, total, layers, rows_dev, dim, hid, emb):
    f32 = jnp.float32
    shards, over = got.shape[0], TAIL
    wide = base.shape[1]
    nr, nc = (hid + emb) // BLK, dim // BLK
    half = layers * nc
    hbm = pl.BlockSpec(memory_space=pl.ANY)
    S = jax.ShapeDtypeStruct

    def of(s):
        t = lax.rem(s, half)
        return t // nc, lax.rem(t, nc)

    def tall(s):
        i, j = of(jnp.minimum(s, half - 1))
        return i, 0, j

    def flat(s):
        i, j = of(jnp.maximum(s, half) - half)
        return i, j, 0

    def block(s):
        i, j = of(s)
        return (2 * i + s // half) * nc + j, 0, 0

    return pl.pallas_call(
        finish_kernel,
        grid=(2 * half,),
        in_specs=[pl.BlockSpec(memory_space=pltpu.SMEM), hbm, hbm, pl.BlockSpec((nr, BLK, BLK), block)],
        out_specs=[hbm, pl.BlockSpec((1, hid, BLK), tall), pl.BlockSpec((1, emb, BLK), tall),
                   pl.BlockSpec((1, BLK, hid), flat), pl.BlockSpec((1, BLK, emb), flat)],
        out_shape=[S((layers, rows_dev, emb), f32), S((layers, hid, dim), f32), S((layers, emb, dim), f32),
                   S((layers, dim, hid), f32), S((layers, dim, emb), f32)],
        scratch_shapes=[pltpu.VMEM((shards, BASE, wide), f32), pltpu.VMEM((layers, shards, over, emb), f32),
                        pltpu.VMEM((layers, rows_dev, emb), f32), pltpu.SemaphoreType.DMA((3,))],
        compiler_params=pltpu.CompilerParams(vmem_limit_bytes=66_000_000),
        name="finish",
    )(got, base.reshape(shards, BASE, wide), tail.reshape(layers, shards, over, emb), total)


WORK = (1, 2, 1, 0, 0)


def tails_kernel(*refs):
    n = len(ORDERS)
    refs = list(refs)

    def take(count):
        return [refs.pop(0) for _ in range(count)]

    (x_in, w_up, w_down, w_gate), tails, outs, rests, (wug, wd), keep = take(4), take(n), take(6), take(n), take(2), take(6)
    (wsem, dsem, ssem, rsem), bufs = take(4), refs
    f32, bf = jnp.float32, jnp.bfloat16
    me = lax.axis_index("emb")
    hid, dim = w_up.shape[2], w_up.shape[1]
    uv, hv, av, mv, zv, gv = keep
    spot = {name: bit(me // w) for name, w in WEIGHT.items()}
    other = {name: me + w - 2 * w * spot[name] for name, w in WEIGHT.items()}
    barrier = pltpu.get_barrier_semaphore()
    for name in AXES:
        pl.semaphore_signal(barrier, inc=1, device_id=(other[name],), device_id_type=MESH)
    cp = pltpu.make_async_copy
    ways = ((w_up, wug.at[:, pl.ds(0, hid)]), (w_down, wd), (w_gate, wug.at[:, pl.ds(hid, w_gate.shape[2])]))
    loads = [cp(src.at[0], dst, wsem.at[i]) for i, (src, dst) in enumerate(ways)]
    for c in loads:
        c.start()
    pl.semaphore_wait(barrier, len(AXES))

    def rows(i):
        return pl.ds(pl.multiple_of(i * TILE, TILE), TILE)

    def put(i):
        return [cp(src.at[rows(i)], dst.at[rows(i)], dsem.at[j, i]) for j, (src, dst) in enumerate(zip(keep, outs))]

    def tile(i):
        r = rows(i)
        x = x_in[r].astype(f32)
        u = (x * lax.rsqrt(jnp.mean(x * x, **ROW) + EPS)).astype(bf)
        uv[r] = u
        for c0 in range(0, hid, FCH):
            c = slice(c0, c0 + FCH)
            h = dot32(u, wug[:, c], NN).astype(bf)
            hv[r, c] = h
            av[r, c] = gelu_f(h.astype(f32)).astype(bf)
        z = dot32(u, wug[:, hid:], NN).astype(bf)
        zv[r] = z
        gv[r] = gelu_f(z.astype(f32)).astype(bf)
        for c0 in range(0, dim, FCH):
            c = slice(c0, c0 + FCH)
            mv[r, c] = dot32(av[r], wd[:, c], NN).astype(bf)
        for c in put(i):
            c.start()

    cur, names = list(tails), [list(AXES) for _ in range(n)]
    first = 0
    for s, count in enumerate(WORK):
        copies, kept = [], []
        for k in range(n):
            name = ORDERS[k][s]
            at = names[k].index(name)
            side = lambda v: tuple(v if i == at else slice(None) for i in range(len(names[k])))
            copies.append(pltpu.make_async_remote_copy(
                src_ref=cur[k].at[side(1 - spot[name])], dst_ref=bufs[s].at[k], send_sem=ssem.at[k, s], recv_sem=rsem.at[k, s],
                device_id=(other[name],), device_id_type=MESH))
            kept.append(side(spot[name]))
            names[k].remove(name)
        for c in copies:
            c.start()
        if s == 0:
            for c in loads:
                c.wait()
        if count:
            loop(first, first + count, tile)
        first += count
        for k in range(n):
            copies[k].wait()
            dst = bufs[len(WORK) + s].at[k] if s + 1 < len(WORK) else rests[k]
            dst[...] = cur[k][kept[k]] + bufs[s][k]
            cur[k] = dst
    for i in range(first):
        for c in put(i):
            c.wait()


def run_tails(x_in, w_up, w_down, w_gate, tails):
    n = len(tails)
    rows, emb = tails[0].shape[1:]
    toks, dim = x_in.shape
    hid = w_up.shape[2]
    bf = jnp.bfloat16
    S, V, D = jax.ShapeDtypeStruct, pltpu.VMEM, pltpu.SemaphoreType.DMA
    hbm, vm = pl.BlockSpec(memory_space=pl.ANY), pl.BlockSpec(memory_space=pltpu.VMEM)
    cube = (2,) * len(AXES)
    keep = [(toks, dim), (toks, hid), (toks, hid), (toks, dim), (toks, emb), (toks, emb)]
    steps = [V((n,) + cube[s + 1:] + (rows, emb), bf) for s in range(len(AXES))]
    sems = [D((3,)), D((len(keep), toks // TILE)), D((n, len(AXES))), D((n, len(AXES)))]
    return pl.pallas_call(
        tails_kernel,
        in_specs=[vm] + [hbm] * 3 + [vm] * n,
        out_specs=[hbm] * len(keep) + [vm] * n,
        out_shape=[S(s, bf) for s in keep] + [S((rows, emb), bf)] * n,
        scratch_shapes=[V((dim, hid + emb), bf), V((hid, dim), bf)] + [V(s, bf) for s in keep] + sems + steps + steps[:-1],
        compiler_params=pltpu.CompilerParams(collective_id=1, has_side_effects=True, vmem_limit_bytes=66_000_000),
        cost_estimate=pl.CostEstimate(flops=10**11, bytes_accessed=10**8, transcendentals=0),
        name="tails",
    )(x_in, w_up, w_down, w_gate, *[t.reshape(cube + (rows, emb)) for t in tails])


def fast_step(got, pick, pick_t, x_in, d_out, ple_tables, w_up, w_down, w_gate, w_proj):
    layers, rows_dev, emb = ple_tables.shape
    shards = got.shape[0]
    served = serve(got, ple_tables, TAIL)
    base = swap(served[0].reshape(shards * BASE, layers * emb))
    u, h, a, m, z, g, *rests = run_tails(x_in, w_up, w_down, w_gate, served[1:])
    x_out, us, as_, ss, os_, dhs, dzs, _, send_b, send_t = run_model(
        (x_in, m, h, z, g), base, rests, pick, pick_t, d_out, w_up, w_down, w_gate, w_proj)
    base = swap(send_b)
    total, tail = reduce_grads(u, a, us, as_, ss, os_, dhs, dzs, send_t)
    table, down, proj, up, gate = finish(got, base, tail, total, layers, rows_dev, w_up.shape[1], w_up.shape[2], emb)
    return x_out, table, up, down, gate, proj


def padded_step(shards, tok_ids, x_in, d_out, ple_tables, w_up, w_down, w_gate, w_proj):
    layers = ple_tables.shape[0]
    rows_dev = ple_tables.shape[1]
    cap_rows = tok_ids.shape[0] // CAP_DIV
    owner_dev = tok_ids // rows_dev
    local_row = tok_ids - owner_dev * rows_dev
    owner_hot = (col(owner_dev) == row(numbers(shards))).astype(jnp.int32)
    slot_rank = jnp.sum((jnp.cumsum(owner_hot, axis=0) - owner_hot) * owner_hot, axis=1)
    dest_slot = owner_dev * cap_rows + slot_rank
    req_send = jnp.zeros((shards * cap_rows,), jnp.int32).at[dest_slot].set(local_row)
    req_recv = swap(req_send)
    x_cur = x_in
    saved_list = []
    rows_list = []
    for layer_idx in range(layers):
        served = jnp.take(ple_tables[layer_idx], req_recv, axis=0)
        returned = swap(served)
        emb_rows = jnp.take(returned, dest_slot, axis=0)
        x_cur, saved = layer_fwd(x_cur, w_up[layer_idx], w_down[layer_idx], w_gate[layer_idx], w_proj[layer_idx], emb_rows)
        saved_list.append(saved)
        rows_list.append(emb_rows)
    d_x = d_out.astype(jnp.float32)
    kept = [None] * layers
    tables_by_layer = [None] * layers
    for layer_idx in reversed(range(layers)):
        d_x, kept[layer_idx], (g, ds) = layer_bwd(d_x, saved_list[layer_idx], rows_list[layer_idx], w_up[layer_idx], w_down[layer_idx], w_gate[layer_idx], w_proj[layer_idx], layer_idx == 0)
        d_rows = g.astype(jnp.float32) * ds.astype(jnp.float32)
        grad_send = jnp.zeros((shards * cap_rows, d_rows.shape[1]), jnp.float32).at[dest_slot].set(d_rows)
        grad_recv = swap(grad_send)
        tables_by_layer[layer_idx] = jax.ops.segment_sum(grad_recv, req_recv, num_segments=rows_dev)
    u, a, s, o, dh, dz = ([k[i] for k in kept] for i in range(6))
    total = reduce_grads(u[0], a[0], jnp.stack(u[1:]), jnp.stack(a[1:]), jnp.stack(s), jnp.stack(o), jnp.stack(dh), jnp.stack(dz), jnp.zeros((TAIL, dz[0].shape[1] * layers), jnp.float32))[0]
    dim, hid, emb = w_up.shape[1], w_up.shape[2], w_gate.shape[2]
    nr, nc = (hid + emb) // BLK, dim // BLK
    total = total.reshape(layers, 2, nr * nc, BLK, BLK)
    tall = total[:, 0].reshape(layers, nc, nr, BLK, BLK).transpose(0, 2, 3, 1, 4).reshape(layers, hid + emb, dim)
    wide = total[:, 1].reshape(layers, nc, nr, BLK, BLK).transpose(0, 1, 3, 2, 4).reshape(layers, dim, hid + emb)
    outs = (x_cur, jnp.stack(tables_by_layer), wide[:, :, :hid], tall[:, :hid], wide[:, :, hid:], tall[:, hid:])
    return tuple(with_layout_constraint(o, Layout(major_to_minor=tuple(range(o.ndim)))) for o in outs)


def solution(mesh):
    shards = mesh.shape["emb"]

    def device_step(tok_ids, *rest):
        tables = rest[2]
        pick, pick_t, got = spread(tok_ids, shards, tables.shape[1])
        fits = jnp.max(got[:, 3]) <= TAIL
        return lax.cond(fits, lambda: fast_step(got, pick, pick_t, *rest), lambda: tuple(padded_step(shards, tok_ids, *rest)))

    return jax.shard_map(
        device_step,
        mesh=mesh,
        in_specs=(P("emb"), P("emb", None), P("emb", None), P(None, "emb", None), P(), P(), P(), P()),
        out_specs=(P("emb", None), P(None, "emb", None), P(), P(), P(), P()),
        check_vma=False,
    )
```

time: 2320 us -> 963 us (0.42)
  waiting for transfers between devices: 1460 us -> 2.98 us
  Pallas kernels: 0 us -> 909 us
  other arithmetic: 291 us -> 12.9 us
  matrix products: 258 us -> 1.41 us
  local copies, waits for them, and re-layouts: 147 us -> 2.33 us
  blocking collectives: 99.4 us -> 0 us
  starting transfers between devices: 48.2 us -> 14.4 us
    pallas_call x0 -> x5, Pallas kernels: none -> 909 us  [the longest x1 638 us: reduce_grads(): pl.pallas_call(functools.partial(reduce_kernel, (n_layers, per, n)), out_...]
    psum x1 -> x0, waiting for transfers between devices: 816 us -> none  [device_step(): grads_by_layer[layer_idx] = lax.psum(grads, 'emb')]
    all_to_all x6 -> x3, waiting for transfers between devices: 640 us -> 2.98 us  [swap(): return lax.all_to_all(a, 'emb', 0, 0, tiled=True)]
    dot_general x33 -> x2, matrix products: 258 us -> 1.41 us  [the longest x1 0.87 us: spread(): want = jnp.dot(pick_t, parts, preferred_element_type=f32)]
    scatter-add x3 -> x0, other arithmetic: 174 us -> none  [device_step(): jax.ops.segment_sum(grad_recv, req_recv, num_segments=rows_dev)]
    gather x6 -> x0, local copies, waits for them, and re-layouts: 122 us -> none  [the longest x3 99.5 us: device_step(): served = jnp.take(ple_tables[layer_idx], req_recv, axis=0)]
    all_to_all x1 -> x0, blocking collectives: 99.4 us -> none  [device_step(): returned = lax.all_to_all(served, 'emb', 0, 0, tiled=True)]
    another operation x8 -> x0, other arithmetic: 72 us -> none  [the longest x4 50.9 us: device_step(): jnp.stack([entry[grad_pos] for entry in grads_by_layer])]
  transfers between devices with their start and end apart: 7 -> 3, of which waited for: 7 -> 1; matrix products, arithmetic and copies ran while one was open for 17% -> 0% of each run, Pallas kernels for 0% -> 73%
where the time goes in v1:
time: 963 us; the launch traced here: 955 us
  Pallas kernels  909 us (94%)
  starting transfers between devices  14.4 us (1%)
  other arithmetic  12.9 us (1%)
    pallas_call x1, Pallas kernels, reduce_grads(): pl.pallas_call(functools.partial(reduce_kernel, (n_layers, per, n)), out_...  638 us
    pallas_call x1, Pallas kernels, run_model(): pl.pallas_call(model_kernel, in_specs=[hbm] * 3 + [vm] * 6 + [hbm] + [vm]...  121 us
    pallas_call x1, Pallas kernels, finish(): pl.pallas_call(finish_kernel, grid=(2 * half,), in_specs=[pl.BlockSpec(me...  70.5 us
    pallas_call x1, Pallas kernels, run_tails(): pl.pallas_call(tails_kernel, in_specs=[vm] + [hbm] * 3 + [vm] * n, out_sp...  62.6 us
  transfers between devices with their start and end apart: 3, of which 1 were waited for; matrix products, arithmetic and copies ran while one was open for 0% of the time, Pallas kernels for 73%

profile of v1, /device:TPU:0, one launch (start us, length us, event | category | flops | bytes accessed | tf_op | source)
XLA Modules:
  0.0 954.9 jit_solution(7960185836895634747)
XLA Ops:
  0.6 0.0 copy-start.30
  0.6 3.7 select_reduce_fusion.1
  4.3 0.7 add_select_fusion.2
  5.0 0.1 select_reduce_fusion.3
  5.2 0.6 fusion.220
  5.8 0.5 fusion.206
  6.3 0.1 select_reduce_fusion.5
  6.4 0.1 select_reduce_fusion.4
  6.5 0.7 add_select_fusion.4
  7.2 1.7 select_reduce_fusion
  9.0 0.9 fusion.201
  9.9 0.1 pad.20.clone
  10.0 0.1 pad.22.clone
  10.1 0.1 slice.104
  10.1 0.7 pad.28.clone
  10.9 0.1 maximum_convert_fusion
  10.9 0.1 copy.87
  11.0 0.7 all_to_all.75
  11.7 7.3 all-to-all-start.9
  19.0 2.5 fusion.200
  21.5 1.9 fusion.202
  23.4 3.0 all-to-all-done.9
  26.4 0.6 copy-done.21
  27.0 0.7 slice_reduce_fusion
  28.3 925.3 %conditional.1 = (bf16[1024,1024]{1,0:T(8,128)(2,1)}, f32[3,4748,256]{2,1,0:T(8,128)}, f32[3,1024,3072]{2,1,0:T(8,128)}, f32[3,3072,1024]{2,1,0:T(8,128)}, f32[3...) conditional(s32[]{:T(128)} %convert_element_type.300, (bf16[1024,1024]{1,0:T(8,128)(2,1)}, ...), branch_computations={%region_9.27_spmd, %region_25.28_spmd} | conditional | flops 699999977472 | bytes 1746183296 | solution.py:1160
  37.5 16.9 %serve_rows.1 = (bf16[32,32,768]{2,1,0:T(8,128)(2,1)}, bf16[32,128,256]{2,1,0:T(8,128)(2,1)}, bf16[32,128,256]{2,1,0:T(8,128)(2,1)}, bf16[32,128,256]{2,1,0:T(8,128)(2,1)}) custom-call(s32[32,288]{1,0:T(8,128)} %get-tuple-element.51.got, bf16[3,4748,256]{2,1,0:T(8,128)(2,1)} %get-tuple-element.52.tables), custom_call_target="tpu_custom_call" | custom-call | tf_op jit(solution)/shard_map/cond/branch_1_fun/serve_rows/pallas_call | solution.py:850
  54.4 3.5 all-to-all-start
  57.9 62.6 %tails.1 = (bf16[1024,1024]{1,0:T(8,128)(2,1)}, bf16[1024,3072]{1,0:T(8,128)(2,1)}, bf16[1024,3072]{1,0:T(8,128)(2,1)}, bf16[1024,1024]{1,0:T(8,128)(2,1)}, bf16...) custom-call(bf16[1024,1024]{1,0:T(8,128)(2,1)} %get-tuple-element.47, ...), custom_call_target="tpu_custom_call" | custom-call | flops 99999997952 | bytes 100000000 | tf_op jit(solution)/shard_map/cond/branch_1_fun/tails/pallas_call | solution.py:1086
  120.5 120.8 %model.1 = (bf16[1024,1024]{1,0:T(8,128)(2,1)}, bf16[2,1024,1024]{2,1,0:T(8,128)(2,1)}, bf16[2,1024,3072]{2,1,0:T(8,128)(2,1)}, bf16[3,1024,256]{2,1,0:T(8,128)(...) custom-call(bf16[1024,1024]{1,0:T(8,128)(2,1)} %get-tuple-element.47, ...), custom_call_target="tpu_custom_call" | custom-call | tf_op jit(solution)/shard_map/cond/branch_1_fun/model/pallas_call | solution.py:722
  241.2 3.5 all-to-all-start.1
  244.8 638.0 %reduce_grads.3 = (f32[312,256,256]{2,1,0:T(8,128)}, f32[3,2,2,2,2,2,128,256]{7,6,5,4,3,2,1,0:T(8,128)}) custom-call(bf16[1024,1024]{1,0:T(8,128)(2,1)} %get-tuple-element.70.refs_0_, bf16[1024,3072]{1,0:T(8,128)(2,1)} %get-tuple-element.71.refs_1_, bf16[2,1024,1024]{2,1,0:T(8,128)(2,1)} %get-tuple-element.72.refs_2_, ...), custom_call_target="tpu_custom_call" | custom-call | flops 599999971328 | bytes 100000000 | tf_op jit(solution)/shard_map/cond/branch_1_fun/reduce_grads/pallas_call | solution.py:439
  882.9 70.5 %finish.1 = (f32[3,4748,256]{2,1,0:T(8,128)}, f32[3,3072,1024]{2,1,0:T(8,128)}, f32[3,256,1024]{2,1,0:T(8,128)}, f32[3,1024,3072]{2,1,0:T(8,128)}, f32[3,1024,256]{2,1,0:T(8,128)}) custom-call(s32[32,288]{1,0:T(8,128)S(1)} %copy-done.22, f32[32,32,768]{2,1,0:T(8,128)} %all-to-all-done.1.base, f32[3,32,128,256]{3,2,1,0:T(8,128)} %bitcast.211, ...), custom_call_target="tpu_custom_call" | custom-call | tf_op jit(solution)/shard_map/cond/branch_1_fun/finish/pallas_call | solution.py:975
  (16 shorter events, 0.1 us)
Async XLA Ops:
  0.6 27.7 %copy-start.30 = (s32[1024]{0:T(1024)S(1)}, s32[1024]{0:T(1024)}, u32[]{:S(2)}) copy-start(s32[1024]{0:T(1024)} %param.14) | copy-start | bytes 12292
  11.7 14.7 %all-to-all-start.9 = ((s32[32,1,288]{2,1,0:T(1,128)}), s32[32,1,288]{2,1,0:T(1,128)S(1)}, u32[]{:S(2)}, u32[]{:S(2)}) async-start(s32[32,1,288]{2,1,0:T(1,128)} %all_to_all.75), calls=%async_computation.9 | async-start | bytes 98304 | tf_op jit(solution)/shard_map/all_to_all | solution.py:85
  26.4 0.6 copy-start.21
  54.4 66.1 %all-to-all-start = ((bf16[32,32,768]{2,1,0:T(8,128)(2,1)}), bf16[32,32,768]{2,1,0:T(8,128)(2,1)}, u32[]{:S(2)}, u32[]{:S(2)}) async-start(bf16[32,32,768]{2,1,0:T(8,128)(2,1)} %get-tuple-element.60), calls=%async_computation | async-start | bytes 3145728 | tf_op jit(solution)/shard_map/cond/branch_1_fun/all_to_all | solution.py:85
  241.2 641.6 %all-to-all-start.1 = ((f32[32,32,768]{2,1,0:T(8,128)}), f32[32,32,768]{2,1,0:T(8,128)}, u32[]{:S(2)}, u32[]{:S(2)}) async-start(f32[32,32,768]{2,1,0:T(8,128)} %bitcast.225), calls=%async_computation.1 | async-start | bytes 6291456 | tf_op jit(solution)/shard_map/cond/branch_1_fun/all_to_all | solution.py:85
  244.8 638.1 %copy-start.22 = (s32[32,288]{1,0:T(8,128)S(1)}, s32[32,288]{1,0:T(8,128)}, u32[]{:S(2)}) copy-start(s32[32,288]{1,0:T(8,128)} %get-tuple-element.51.got) | copy-start | bytes 110596 | tf_op jit(solution)/shard_map/cond

commit v2 on v1

--- a/solution.py
+++ b/solution.py
@@ -57,9 +57,13 @@
     return d_x_new, (normed, act_out, mix_rows, g_out, d_hidden, d_gate_pre), (gate_act, d_mix)
 
 
+BASE = 32
+TAIL = 128
 AXES = ("far", "near", "y", "x", "core")
 WEIGHT = {name: 1 << i for i, name in enumerate(reversed(AXES))}
 ORDERS = (("core", "x", "y", "near", "far"), ("core", "y", "near", "x", "far"), ("core", "near", "x", "y", "far"))
+DOUBLING = [tuple(reversed(order)) for order in ORDERS]
+PARTS = ((0, 48), (48, 40), (88, 40))
 MESH = pl.DeviceIdType.MESH
 DEPTH = 2
 FIRST = range(DEPTH)
@@ -67,6 +71,8 @@
 NN, NT, TN = ((1,), (0,)), ((1,), (1,)), ((0,), (0,))
 ROW = {"axis": -1, "keepdims": True}
 HALF, QUART, EIGHTH = 128, 64, 32
+COST = pl.CostEstimate(flops=10**11, bytes_accessed=10**8, transcendentals=0)
+VMEM_LIMIT = 66_000_000
 
 
 def bit(v):
@@ -112,20 +118,16 @@
     (v_as, v_o, v_u, v_d, blk1, blk2, blk3, rc1, rc2, rc3, rf1, rf2, rs1, rs2, ri1, ri2, rm1, rm2, fin1, fin2,
      ri3, rm3, rx3, rf3, rs3, fin3, ssem, rsem, lsem, osem, tv, tsem, trsem, tlsem) = refs[11:]
     me = lax.axis_index("emb")
-    core, x, y, z = bit(me), bit(me // 2), bit(me // 4), me // 8
-    mid = (z == 1) | (z == 2)
-    end = (z == 0) | (z == 3)
-    zb = z // 2
-    p_core = me + 1 - 2 * core
-    p_x = me + 2 - 4 * x
-    p_y = me + 4 - 8 * y
-    step_in = jnp.where((z == 0) | (z == 1), 8, -8)
-    p_side = jnp.where((z == 0) | (z == 2), me + 8, me - 8)
-    p_mid = jnp.where(z == 1, me + 8, jnp.where(z == 2, me - 8, me))
+    spot = {name: bit(me // w) for name, w in WEIGHT.items()}
+    other = {name: me + w - 2 * w * spot[name] for name, w in WEIGHT.items()}
+    core, x, y, zb, near = (spot[name] for name in ("core", "x", "y", "far", "near"))
+    p_core, p_x, p_y, p_side = (other[name] for name in ("core", "x", "y", "near"))
+    mid = near != zb
+    end = near == zb
+    p_mid = me + WEIGHT["near"] * (near - zb)
 
     barrier = pltpu.get_barrier_semaphore()
-    p_far = me + 16 - EIGHTH * zb
-    for dev in (p_core, p_x, p_y, p_side, p_far):
+    for dev in other.values():
         pl.semaphore_signal(barrier, inc=1, device_id=(dev,), device_id_type=MESH)
 
     @pl.when(mid)
@@ -148,32 +150,20 @@
                 (dh, v_d.at[slot, :, left]), (dz, v_d.at[slot, :, right]))
         return [pltpu.make_async_copy(src, dst, osem.at[slot, i]) for i, (src, dst) in enumerate(ways)]
 
-    emb = tv.shape[2]
-    spot = {"far": z // 2, "near": bit(z), "y": y, "x": x, "core": core}
-    other = {"far": p_far, "near": p_side, "y": p_y, "x": p_x, "core": p_core}
-    t_half = tv.shape[1] // 2
-
-    def tail_copy(layer, s, p):
-        order = tuple(reversed(ORDERS[layer]))
-        block = p // 2
-        at = {name: bit(block // (1 << t)) for t, name in enumerate(order[:s])}
-        where = tuple(at.get(name, spot[name]) for name in AXES)
-        ref = tails.at[(layer,) + where + (pl.ds(pl.multiple_of(bit(p) * t_half, t_half), t_half),)]
-        i = lax.rem(p, 4)
-        return pltpu.make_async_remote_copy(src_ref=ref, dst_ref=ref, send_sem=tsem.at[layer, s, i], recv_sem=trsem.at[layer, s, i],
+    def tail_copy(part, s, p):
+        order = DOUBLING[part]
+        at = {name: bit(p // (1 << t)) for t, name in enumerate(order[:s])}
+        ref = tails.at[tuple(at.get(name, spot[name]) for name in AXES) + (pl.ds(*PARTS[part]),)]
+        i = lax.rem(p, LAG + LAG)
+        return pltpu.make_async_remote_copy(src_ref=ref, dst_ref=ref, send_sem=tsem.at[part, s, i], recv_sem=trsem.at[part, s, i],
                                             device_id=(other[order[s]],), device_id_type=MESH)
 
     t_first = [4]
     for s in range(len(AXES)):
-        t_first.append(t_first[-1] + (2 << s) + 2)
-    t_in = [pltpu.make_async_copy(send_t.at[:, pl.ds(k * emb, emb)], tv.at[k], tlsem.at[k]) for k in range(n_layers)]
-    t_own = [pltpu.make_async_copy(tv.at[k], tails.at[(k,) + tuple(spot[name] for name in AXES)], tlsem.at[k]) for k in range(n_layers)]
-    for c in t_in:
+        t_first.append(t_first[-1] + (1 << s) + 2)
+    t_own = pltpu.make_async_copy(send_t, tv, tlsem.at[0]), pltpu.make_async_copy(tv, tails.at[tuple(spot[name] for name in AXES)], tlsem.at[0])
+    for c in t_own:
         c.start()
-    for c, d in zip(t_in, t_own):
-        c.wait()
-        d.start()
-    for c in t_own:
         c.wait()
     for ell in (0, 1):
         for c in loads(ell):
@@ -183,16 +173,17 @@
 
     span = n // n_layers
     rest = {0: 2, 1: 4}
+    early, close = 4, 10
 
     def active(k, kind):
-        return True if kind == 2 else lax.rem(k, 5) != rest[kind]
+        return k < n - early if kind == 2 else (lax.rem(k, 5) != rest[kind]) | (k >= n - close)
 
     def unit(k, kind):
         t = lax.rem(k, span)
         if kind == 2:
-            return span * 4 // 5 + t // 2
+            return span * 4 // 5 + jnp.where(k >= n - span, early // 2, 0) + t // 2
         p = lax.rem(t, 5)
-        return 4 * (t // 5) + p - (p > rest[kind]).astype(jnp.int32)
+        return jnp.where(k >= n - close, t - close + 4, 4 * (t // 5) + p - (p > rest[kind]).astype(jnp.int32))
 
     def where_out(k, kind):
         base = {0: 0, 1: per, 2: per * bit(k)}[kind]
@@ -282,7 +273,9 @@
         at = clock()
         odd = lambda k: bit(k) == 1
         at_end = lambda k: bit(k // 2) == 1
-        here = lambda k: jnp.where(at_end(k), end, mid)
+        go = lambda k: active(k, kind)
+        here = lambda k: go(k) & jnp.where(at_end(k), end, mid)
+        on = lambda side: (lambda k: side & go(k))
         q0, q1 = h0 + zb * QUART, h0 + (1 - zb) * QUART
         b = lambda k: lax.rem(k, NB)
         m = lambda k: lax.rem(k, NS)
@@ -292,28 +285,28 @@
         e1 = lambda k: q0 + (1 - f(k)) * EIGHTH
         p_f = lambda k: jnp.where(odd(k), p_y, p_x)
         p_s = lambda k: jnp.where(odd(k), p_x, p_y)
-        e_root = lambda side: (lambda k: side & at_end(k))
-        m_root = lambda side: (lambda k: side & jnp.logical_not(at_end(k)))
-        f_core = add_flow(at(), lambda k: blk.at[b(k), rows(HALF - h0, HALF)], lambda k: rc.at[m(k)], p_core)
+        e_root = lambda side: (lambda k: side & go(k) & at_end(k))
+        m_root = lambda side: (lambda k: side & go(k) & jnp.logical_not(at_end(k)))
+        f_core = add_flow(at(), lambda k: blk.at[b(k), rows(HALF - h0, HALF)], lambda k: rc.at[m(k)], p_core, go, go)
         f_in = add_flow(at(), lambda k: blk.at[b(k), rows(h0, HALF)], lambda k: ri.at[b(k)], p_side, m_root(end), m_root(mid))
         f_in2 = add_flow(at(0), lambda k: blk.at[b(k), rows(q1, QUART)], lambda k: ri.at[b(k), pl.ds(0, QUART)], p_side, e_root(end), e_root(mid))
-        f_mid = add_flow(at(), lambda k: blk.at[b(k), rows(q1, QUART)], lambda k: rm.at[m(k)], p_mid, mid, mid)
+        f_mid = add_flow(at(), lambda k: blk.at[b(k), rows(q1, QUART)], lambda k: rm.at[m(k)], p_mid, on(mid), on(mid))
         f_x = add_flow(at(), lambda k: blk.at[b(k), rows(q0, QUART)], lambda k: rx.at[m(k)], p_side, e_root(mid), e_root(end))
         f_first = add_flow(at(), lambda k: blk.at[b(k), rows(e1(k), EIGHTH)], lambda k: rf.at[m(k)], p_f, here, here)
         f_second = add_flow(at(), lambda k: blk.at[b(k), rows(e0(k), EIGHTH)], lambda k: rs.at[m(k)], p_s, here, here)
         g_f = add_flow(at(), lambda k: fin.at[m(k)], lambda k: out.at[o(k), rows(e0(k), EIGHTH)], p_f, here, here)
         g_x = add_flow(at(), lambda k: out.at[o(k), rows(q0, QUART)], lambda k: out.at[o(k), rows(q0, QUART)], p_side, e_root(end), e_root(mid))
-        g_m = add_flow(at(), lambda k: out.at[o(k), rows(q0, QUART)], lambda k: out.at[o(k), rows(q0, QUART)], p_mid, mid, mid)
+        g_m = add_flow(at(), lambda k: out.at[o(k), rows(q0, QUART)], lambda k: out.at[o(k), rows(q0, QUART)], p_mid, on(mid), on(mid))
         g_o = add_flow(at(), lambda k: out.at[o(k), rows(h0, HALF)], lambda k: out.at[o(k), rows(h0, HALF)], p_side, m_root(mid), m_root(end))
         g_o2 = add_flow(at(0), lambda k: out.at[o(k), rows(q1, QUART)], lambda k: out.at[o(k), rows(q1, QUART)], p_side, e_root(mid), e_root(end))
-        g_c = add_flow(at(), lambda k: out.at[o(k), rows(h0, HALF)], lambda k: out.at[o(k), rows(h0, HALF)], p_core)
+        g_c = add_flow(at(), lambda k: out.at[o(k), rows(h0, HALF)], lambda k: out.at[o(k), rows(h0, HALF)], p_core, go, go)
 
         def plus(start, size, src):
-            def go(k):
+            def add(k):
                 r = rows(start(k), size)
                 blk[b(k), r] = blk[b(k), r] + src(k)
 
-            return go
+            return add
 
         def final(k):
             fin[m(k)] = blk[b(k), rows(e0(k), EIGHTH)] + rs[m(k)]
@@ -359,15 +352,15 @@
         for s in range(len(AXES)):
             p = r - t_first[s]
 
-            @pl.when((p >= 2) & (p < (2 << s) + 2))
+            @pl.when((p >= 2) & (p < (1 << s) + 2))
             def _(s=s, p=p):
-                for k in range(n_layers):
-                    tail_copy(k, s, p - 2).wait()
-
-            @pl.when((p >= 0) & (p < (2 << s)))
+                for part in range(len(PARTS)):
+                    tail_copy(part, s, p - 2).wait()
+
+            @pl.when((p >= 0) & (p < (1 << s)))
             def _(s=s, p=p):
-                for k in range(n_layers):
-                    tail_copy(k, s, p).start()
+                for part in range(len(PARTS)):
+                    tail_copy(part, s, p).start()
         for ell in range(1, n_layers):
             @pl.when(r == span * ell)
             def _(ell=ell):
@@ -399,11 +392,11 @@
         def _():
             blk2[s] = block(slot, unit(r, 1), True)
 
-        @pl.when((r < n) & odd)
+        @pl.when((r < n) & active(r, 2) & odd)
         def _():
             blk3[s] = block(slot, unit(r, 2), True)
 
-        @pl.when((r < n) & jnp.logical_not(odd))
+        @pl.when((r < n) & active(r, 2) & jnp.logical_not(odd))
         def _():
             blk3[s] = block(slot, unit(r, 2), False)
 
@@ -413,7 +406,7 @@
                 for c in loads(ell):
                     c.start()
 
-    loop(0, n + 25, round_)
+    loop(0, n + 22, round_)
 
 
 def reduce_grads(u_0, a_0, us, as_, ss, os_, dhs, dzs, send_t):
@@ -434,17 +427,17 @@
     scratch += many(1, NB, HALF) + many(DEPTH, NS, QUART) + many(3, NS, EIGHTH)
     D = pltpu.SemaphoreType.DMA
     scratch += [D((31, NB)), D((31, NB)), D((3, NS)), D((DEPTH, 6))]
-    scratch += [V((n_layers, over, emb), f32)] + [D((n_layers, len(AXES), LAG + LAG))] * DEPTH + [D((n_layers,))]
+    scratch += [V((over, emb), f32)] + [D((len(PARTS), len(AXES), LAG + LAG))] * DEPTH + [D((1,))]
     flat = (u_0, a_0, us, as_, ss, os_, dhs, dzs, send_t)
     return pl.pallas_call(
         functools.partial(reduce_kernel, (n_layers, per, n)),
         out_shape=[jax.ShapeDtypeStruct((2 * per * n_layers, BLK, BLK), f32),
-                   jax.ShapeDtypeStruct((n_layers,) + (2,) * len(AXES) + (over, emb), f32)],
+                   jax.ShapeDtypeStruct((2,) * len(AXES) + (over, emb), f32)],
         in_specs=[pl.BlockSpec(memory_space=pl.ANY)] * len(flat),
         out_specs=[pl.BlockSpec(memory_space=pl.ANY)] * 2,
         scratch_shapes=scratch,
-        compiler_params=pltpu.CompilerParams(collective_id=0, has_side_effects=True, vmem_limit_bytes=66_000_000),
-        cost_estimate=pl.CostEstimate(flops=600 * 10**9, bytes_accessed=10**8, transcendentals=0),
+        compiler_params=pltpu.CompilerParams(collective_id=0, has_side_effects=True, vmem_limit_bytes=VMEM_LIMIT),
+        cost_estimate=COST,
         name="reduce_grads",
     )(*flat)
 
@@ -467,9 +460,9 @@
 
 def model_kernel(*refs):
     (x0, m0, h0, z0, g0, base, t0, t1, t2, pick, pick_t, d_out, w_up, w_down, w_gate, w_proj,
-     x_out, us, as_, ss, os_, dhs, dzs, hs, send_b, send_t,
+     x_out, us, as_, ss, os_, dhs, dzs, hs, base_in, tails_in, send_b, send_t,
      wug, wd, wp, wp0, xs, cs, hbuf, abuf, ubuf, obuf, pbuf, sbuf, zs, es, gs, invs, dus, dsv, sb, st,
-     wsem, usem, hsem, asem, osem, isem, jsem, psem, ssem, zsem, vsem) = refs
+     wsem, usem, hsem, asem, osem, isem, jsem, psem, ssem, zsem, vsem, bsem, tsem, rsem, trsem) = refs
     f32, bf = jnp.float32, jnp.bfloat16
     slots = base.shape[0]
     n_tiles = xs.shape[1] // TILE
@@ -489,6 +482,61 @@
         return dot32(a, b, NT)
 
     cp = pltpu.make_async_copy
+    me = lax.axis_index("emb")
+    devices = slots // BASE
+    peers = range(1, devices)
+    barrier = pltpu.get_barrier_semaphore()
+    for d in peers:
+        pl.semaphore_signal(barrier, inc=1, device_id=(lax.rem(me + d, devices),), device_id_type=MESH)
+
+    def parcel(slot, d):
+        dev = lax.rem(me + d, devices)
+        return pltpu.make_async_remote_copy(
+            src_ref=sb.at[slot, pl.ds(pl.multiple_of(dev * BASE, BASE), BASE)], dst_ref=base_in.at[1 - slot, me],
+            send_sem=bsem.at[slot, d], recv_sem=rsem.at[slot, d], device_id=(dev,), device_id_type=MESH)
+
+    spots = {name: bit(me // w) for name, w in WEIGHT.items()}
+
+    def tail_copies(layer, s):
+        below = layer - 1
+        copies = []
+        for part, order in enumerate(DOUBLING):
+            ref = tails_in.at[(below,) + tuple(slice(None) if name in order[:s] else spots[name] for name in AXES) + (pl.ds(*PARTS[part]),)]
+            w = WEIGHT[order[s]]
+            copies.append(pltpu.make_async_remote_copy(
+                src_ref=ref, dst_ref=ref, send_sem=tsem.at[below, s, part], recv_sem=trsem.at[below, s, part],
+                device_id=(me + w - 2 * w * spots[order[s]],), device_id_type=MESH))
+        return copies
+
+    def tail_wait(layer, s):
+        for c in tail_copies(layer, s):
+            c.wait()
+
+    def tail_start(layer, s):
+        if s:
+            tail_wait(layer, s - 1)
+        for c in tail_copies(layer, s):
+            c.start()
+
+    plan = {"bwd2": "222.", "bwd1": "2111", "bwd0": ".1.."}
+    begun = dict.fromkeys("12", 1)
+
+    def steps_of(name):
+        steps = []
+        for at, which in enumerate(plan.get(name, "")):
+            if which in begun:
+                steps.append((at, int(which), begun[which]))
+                begun[which] += 1
+        return steps
+
+    def at_tile(i, steps):
+        for at, which, s in steps:
+            @pl.when(i == at)
+            def _(which=which, s=s):
+                tail_start(which, s)
+
+    def own(slot):
+        return cp(sb.at[slot, pl.ds(pl.multiple_of(me * BASE, BASE), BASE)], base_in.at[1 - slot, me], vsem.at[slot])
 
     def weights(layer, slot):
         ways = ((w_up, wug.at[slot, :, pl.ds(0, hid)]), (w_down, wd.at[slot]), (w_gate, wug.at[slot, :, pl.ds(hid, emb)]), (w_proj, wp.at[slot]))
@@ -555,6 +603,60 @@
     loop(0, n_tiles, finish0)
     for i in ends:
         put_s(0)(i).wait()
+
+    def in_d(i):
+        return cp(d_out.at[rows(i)], ubuf.at[slot_of(i)], isem.at[slot_of(i)])
+
+    def put_t(layer):
+        below = layer - 1
+        dst = tails_in.at[(below,) + tuple(spots[name] for name in AXES)] if layer else send_t
+        return cp(st, dst, jsem.at[0])
+
+    def rows_back(layer, slot):
+        below = layer - 1
+        proj = wp0 if layer == 0 else wp.at[slot]
+        if layer == top:
+            for i in FIRST:
+                in_d(i).start()
+
+        def tile(i):
+            r = rows(i)
+            if layer == top:
+                in_d(i).wait()
+                cs[r] = ubuf[slot_of(i)].astype(f32)
+
+                @pl.when(i + DEPTH < n_tiles)
+                def _():
+                    in_d(i + DEPTH).start()
+            dsv[r] = mt(cs[r].astype(bf), proj[...]).astype(bf)
+
+        loop(0, n_tiles, tile)
+        g = g0 if layer == 0 else gs.at[below]
+        d = g[...].astype(f32) * dsv[...].astype(f32)
+        high = d.astype(bf)
+        low = (d - high.astype(f32)).astype(bf)
+        spot = layer % 2
+        if layer == 0:
+            for d in peers:
+                parcel(spot, d).wait_send()
+            own(spot).wait()
+        for c0 in range(0, slots, BLK):
+            p = pick_t[c0:c0 + BLK]
+            sb[spot, c0:c0 + BLK] = mm(p, high) + mm(p, low)
+        p = pick_t[slots:]
+        st[...] = mm(p, high) + mm(p, low)
+        put_t(layer).start()
+        if layer == 0:
+            cp(sb.at[spot], send_b, vsem.at[spot]).start()
+        else:
+            own(spot).start()
+            if layer == top:
+                pl.semaphore_wait(barrier, devices - 1)
+            put_t(layer).wait()
+            tail_start(layer, 0)
+            if layer == top:
+                for d in peers:
+                    parcel(spot, d).start()
 
     def fwd(layer, slot, loaded):
         below = layer - 1
@@ -567,6 +669,20 @@
         for i in FIRST:
             in_p(i).start()
 
+        def gates(i):
+            r = rows(i)
+            x = xs[below, r].astype(f32)
+            inv = lax.rsqrt(jnp.mean(x * x, **ROW) + EPS)
+            invs[below, r] = jnp.broadcast_to(inv, (TILE, invs.shape[2]))
+            z = mm((x * inv).astype(bf), wug[slot, :, hid:]).astype(bf)
+            zs[below, r] = z
+            gs[below, r] = gelu_f(z.astype(f32)).astype(bf)
+
+        loop(0, n_tiles, gates)
+        if layer == top:
+            rows_back(layer, slot)
+        steps = steps_of(f"fwd{layer}")
+
         def tile(i):
             r, k = rows(i), slot_of(i)
 
@@ -575,19 +691,15 @@
                 for o in outs:
                     o(i - DEPTH).wait()
 
+            at_tile(i, steps)
             x = xs[below, r].astype(f32)
-            inv = lax.rsqrt(jnp.mean(x * x, **ROW) + EPS)
-            invs[below, r] = jnp.broadcast_to(inv, (TILE, invs.shape[2]))
-            u = (x * inv).astype(bf)
+            u = (x * invs[below, r][:, :1]).astype(bf)
             ubuf[k] = u
             for c0 in range(0, hid, FCH):
                 h = mm(u, wug[slot, :, c0:c0 + FCH]).astype(bf)
                 hbuf[k, :, c0:c0 + FCH] = h
                 abuf[k, :, c0:c0 + FCH] = gelu_f(h.astype(f32)).astype(bf)
-            z = mm(u, wug[slot, :, hid:]).astype(bf)
-            g = gelu_f(z.astype(f32)).astype(bf)
-            zs[below, r] = z
-            gs[below, r] = g
+            g = gs[below, r]
             e = rows_of(layer, i)
             es[layer, r] = e
             s = (g.astype(f32) * e.astype(f32)).astype(bf)
@@ -622,15 +734,12 @@
         outs = [lambda i: cp(abuf.at[slot_of(i), :, pl.ds(0, hid)], dhs.at[layer, rows(i)], asem.at[slot_of(i)]),
                 lambda i: cp(abuf.at[slot_of(i), :, pl.ds(hid, emb)], dzs.at[layer, rows(i)], zsem.at[slot_of(i)]),
                 put(obuf, os_, layer, osem)]
-        proj = wp0 if layer == 0 else wp.at[slot]
-
-        def in_d(i):
-            return cp(d_out.at[rows(i)], ubuf.at[slot_of(i)], isem.at[slot_of(i)])
-
+        steps = steps_of(f"bwd{layer}")
         if layer == top:
             for i in FIRST:
                 in_h(layer, i).start()
-                in_d(i).start()
+        else:
+            rows_back(layer, slot)
 
         def tile(i):
             r, k = rows(i), slot_of(i)
@@ -640,13 +749,15 @@
                 for o in outs:
                     o(i - DEPTH).wait()
 
-            if layer == top:
-                in_d(i).wait()
-                cs[r] = ubuf[k].astype(f32)
+            at_tile(i, steps)
+            if layer == 1:
+                @pl.when(i == n_tiles - 1)
+                def _():
+                    for d in peers:
+                        parcel(layer, d).start()
             o = cs[r].astype(bf)
             obuf[k] = o
-            ds = mt(o, proj[...]).astype(bf)
-            dsv[r] = ds
+            ds = dsv[r]
             z = (z0[r] if layer == 0 else zs[below, r]).astype(f32)
             dg = (es[layer, r].astype(f32) * ds.astype(f32)).astype(bf)
             abuf[k, :, hid:] = gelu_g(z, dg.astype(f32)).astype(bf)
@@ -671,31 +782,14 @@
             @pl.when(i + DEPTH < n_tiles)
             def _():
                 in_h(layer, i + DEPTH).start()
-                if layer == top:
-                    in_d(i + DEPTH).start()
 
         loop(0, n_tiles, tile)
         if layer > 0:
             for i in FIRST:
                 in_h(below, i).start()
-        g = g0 if layer == 0 else gs.at[below]
-        d = g[...].astype(f32) * dsv[...].astype(f32)
-        high = d.astype(bf)
-        low = (d - high.astype(f32)).astype(bf)
-        for c0 in range(0, slots, 256):
-            p = pick_t[c0:c0 + 256]
-            sb[c0:c0 + 256] = mm(p, high) + mm(p, low)
-        p = pick_t[slots:]
-        st[...] = mm(p, high) + mm(p, low)
-        lanes = slice(layer * emb, (layer + 1) * emb)
-        both = [cp(sb, send_b.at[:, lanes], vsem.at[0]), cp(st, send_t.at[:, lanes], vsem.at[1])]
-        for c in both:
-            c.start()
         for i in ends:
             for o in outs:
                 o(i).wait()
-        for c in both:
-            c.wait()
 
     fwd(1, 0, w1)
     fwd(2, 1, w2)
@@ -705,6 +799,14 @@
     bwd(1, 0)
     last.wait()
     bwd(0, 1)
+    put_t(0).wait()
+    for layer in (1, 2):
+        tail_wait(layer, len(AXES) - 1)
+    cp(sb.at[0], send_b, vsem.at[0]).wait()
+    own(1).wait()
+    for d in peers:
+        parcel(0, d).wait_recv()
+        parcel(1, d).wait()
 
 
 def run_model(pre, base, tails, pick, pick_t, d_out, w_up, w_down, w_gate, w_proj):
@@ -722,24 +824,21 @@
     return pl.pallas_call(
         model_kernel,
         in_specs=[hbm] * 3 + [vm] * 6 + [hbm] + [vm] + [hbm] * 5,
-        out_specs=[hbm] * 10,
+        out_specs=[hbm] * 12,
         out_shape=[S((toks, dim), bf), S((below, toks, dim), bf), S((below, toks, hid), bf), S((layers, toks, emb), bf),
                    S((layers, toks, dim), bf), S((layers, toks, hid), bf), S((layers, toks, emb), bf), S((below, toks, hid), bf),
-                   S((slots, layers * emb), f32), S((over, layers * emb), f32)],
+                   S((below, slots // BASE, BASE, emb), f32),
+                   S((below,) + (2,) * len(AXES) + (over, emb), f32), S((slots, emb), f32), S((over, emb), f32)],
         scratch_shapes=[
             V((DEPTH, dim, hid + emb), bf), V((DEPTH, hid, dim), bf), V((DEPTH, emb, dim), bf), V((emb, dim), bf),
             V((DEPTH, toks, dim), bf), V((toks, dim), f32), V((DEPTH, TILE, hid), bf), V((DEPTH, TILE, hid + emb), bf),
             V((DEPTH, TILE, dim), bf), V((DEPTH, TILE, dim), bf), V((DEPTH, TILE, slots + over), bf), V((DEPTH, TILE, emb), bf),
             V((DEPTH, toks, emb), bf), V((layers, toks, emb), bf), V((DEPTH, toks, emb), bf), V((DEPTH, toks, 128), f32), V((TILE, dim), f32),
-            V((toks, emb), bf), V((slots, emb), f32), V((over, emb), f32),
-            D((DEPTH, 5))] + [D((DEPTH,))] * 10,
-        compiler_params=pltpu.CompilerParams(vmem_limit_bytes=67_000_000),
+            V((toks, emb), bf), V((DEPTH, slots, emb), f32), V((over, emb), f32),
+            D((DEPTH, 5))] + [D((DEPTH,))] * 10 + [D((DEPTH, slots // BASE)), D((DEPTH, len(AXES), len(PARTS)))] * DEPTH,
+        compiler_params=pltpu.CompilerParams(collective_id=2, has_side_effects=True, vmem_limit_bytes=VMEM_LIMIT),
         name="model",
     )(x0, m0, h0, z0, g0, base, *tails, pick, pick_t, d_out, w_up, w_down, w_gate, w_proj)
-
-
-BASE = 32
-TAIL = 128
 
 
 def spread(tok_ids, shards, rows_dev):
@@ -750,8 +849,11 @@
     row_no = lax.broadcasted_iota(i32, (toks, toks), 0)
     col_no = lax.broadcasted_iota(i32, (toks, toks), 1)
     same = col(tok_ids) == row(tok_ids)
-    seen = jnp.max(jnp.where(same & (col_no < row_no), 1.0, 0.0), axis=1)
-    new = 1.0 - seen
+
+    def first_one(earlier, axis):
+        return 1.0 - jnp.max((same & earlier).astype(f32), axis=axis)
+
+    new = first_one(col_no < row_no, 1)
     hot32 = (col(owner) == row(numbers(shards))).astype(f32)
     fresh = hot32 * col(new)
     before = (row_no > col_no).astype(bf)
@@ -763,8 +865,8 @@
     start = jnp.sum(jnp.where(lower, row(extra), 0.0), axis=1)
     tail = jnp.sum(hot32 * row(start), axis=1)
     place = jnp.where(rank < BASE, owner.astype(f32) * BASE + rank, shards * BASE + tail + rank - BASE)
-    row_new = jnp.max(jnp.where(same & (row_no < col_no), 1.0, 0.0), axis=0) == 0.0
-    slot = jnp.sum(jnp.where(same & row(row_new), row(place), 0.0), axis=1).astype(i32)
+    spots = place * first_one(row_no < col_no, 0)
+    slot = jnp.sum(same.astype(f32) * row(spots), axis=1).astype(i32)
     n_slots = shards * BASE + TAIL
     pick = (col(slot) == lax.broadcasted_iota(i32, (toks, n_slots), 1)).astype(bf)
     pick_t = (row(slot) == lax.broadcasted_iota(i32, (n_slots, toks), 0)).astype(bf)
@@ -773,7 +875,9 @@
     want = (want[:, 0] * 64.0 + want[:, 1]).astype(i32)
     base = want[:shards * BASE].reshape(shards, BASE)
     rest = jnp.broadcast_to(want[shards * BASE:][None, :], (shards, TAIL))
-    info = jnp.stack([count, start, extra, jnp.broadcast_to(jnp.sum(extra), (shards,))], axis=1).astype(i32)
+    total = jnp.sum(extra)
+    fit = (total <= TAIL).astype(f32)
+    info = jnp.stack([count, start * fit, extra * fit, jnp.broadcast_to(total, (shards,))], axis=1).astype(i32)
     pad = jnp.zeros((shards, INFO - 4), i32)
     sent = jnp.concatenate([info, pad, base, rest], axis=1)
     got = swap(sent)
@@ -801,6 +905,8 @@
         loop(0, whole // BLK, widen)
         wide[k, whole:] = tab[k, whole:].astype(jnp.float32)
 
+    stage[...] = jnp.zeros_like(stage)
+
     def one(j):
         start, extra = got[j, 1], got[j, 2]
 
@@ -810,7 +916,8 @@
                 for k in range(n_layers):
                     stage[k, line(g * 8 + i)] = wide[k, line(at[i])]
 
-        loop(0, BASE // 8, rows8)
+        used = jnp.minimum(got[j, 0], BASE)
+        loop(0, (used + 7) // 8, rows8)
         for k in range(n_layers):
             base_out[j, :, k * emb:(k + 1) * emb] = stage[k, :BASE].astype(jnp.bfloat16)
 
@@ -854,7 +961,7 @@
         out_shape=shapes,
         scratch_shapes=[pltpu.VMEM((n_layers, rows_dev, emb), bf), pltpu.VMEM((n_layers, rows_dev, emb), jnp.float32),
                         pltpu.VMEM((n_layers, over, emb), jnp.float32), pltpu.SemaphoreType.DMA((n_layers,))],
-        compiler_params=pltpu.CompilerParams(vmem_limit_bytes=60_000_000),
+        compiler_params=pltpu.CompilerParams(vmem_limit_bytes=VMEM_LIMIT),
         name="serve_rows",
     )(got, tables)
 
@@ -862,20 +969,21 @@
 STEPS = 24
 
 
-def finish_kernel(got, base, tail, total, table, down, proj, up, gate, base_v, tail_v, acc, sem):
+def finish_kernel(got, base, base_in, tail, tails_in, total, table, down, proj, up, gate, base_v, tail_v, acc, sem):
     step = pl.program_id(0)
     shards = got.shape[0]
     n_layers, _, emb = acc.shape
-    first = pltpu.make_async_copy(base, base_v, sem.at[0])
-    second = pltpu.make_async_copy(tail, tail_v, sem.at[1])
+    first = [pltpu.make_async_copy(base, base_v.at[0], sem.at[0]),
+             pltpu.make_async_copy(base_in, base_v.at[pl.ds(1, n_layers - 1)], sem.at[3])]
+    second = [pltpu.make_async_copy(tail, tail_v.at[0], sem.at[1]),
+              pltpu.make_async_copy(tails_in, tail_v.at[pl.ds(1, n_layers - 1)], sem.at[4])]
     done = pltpu.make_async_copy(acc, table, sem.at[2])
     n = total.shape[0] - 1
-    lanes = [slice(k * emb, (k + 1) * emb) for k in range(n_layers)]
 
     @pl.when(step == 0)
     def _():
-        first.start()
-        second.start()
+        for c in first + second:
+            c.start()
         whole = acc.shape[1] // BLK * BLK
         for k in range(n_layers):
             def clear(i, k=k):
@@ -883,7 +991,8 @@
 
             loop(0, whole // BLK, clear)
             acc[k, whole:] = jnp.zeros((acc.shape[1] - whole, emb), jnp.float32)
-        first.wait()
+        for c in first:
+            c.wait()
 
     @pl.when(step < STEPS // 2)
     def _():
@@ -902,9 +1011,9 @@
             at = [line(got[j, INFO + g * 8 + i]) for i in range(8)]
             for i in range(8):
                 for k in range(n_layers):
-                    acc[k, at[i]] = acc[k, at[i]] + base_v[j, line(g * 8 + i), lanes[k]]
-
-        loop(0, BASE // 8, rows8)
+                    acc[k, at[i]] = acc[k, at[i]] + base_v[k, j, line(g * 8 + i)]
+
+        loop(0, (jnp.minimum(got[j, 0], BASE) + 7) // 8, rows8)
 
     def two(j):
         start, extra = got[j, 1], got[j, 2]
@@ -924,21 +1033,23 @@
         loop(0, extra // 4, four)
         loop(extra // 4 * 4, extra, single)
 
-    part = shards // 8
-
-    @pl.when(step < 8)
+    turn = STEPS // 2
+    part = 4
+
+    @pl.when(step < turn)
     def _():
-        loop(step * part, (step + 1) * part, one)
-
-    @pl.when(step == 8)
+        loop(step * part, jnp.minimum((step + 1) * part, shards), one)
+
+    @pl.when(step == turn)
     def _():
-        second.wait()
-
-    @pl.when((step >= 8) & (step < 16))
+        for c in second:
+            c.wait()
+
+    @pl.when(step >= turn)
     def _():
-        loop((step - 8) * part, (step - 7) * part, two)
-
-    @pl.when(step == 17)
+        loop(jnp.minimum((step - turn) * part, shards), jnp.minimum((step - turn + 1) * part, shards), two)
+
+    @pl.when(step == STEPS - 5)
     def _():
         done.start()
 
@@ -947,10 +1058,9 @@
         done.wait()
 
 
-def finish(got, base, tail, total, layers, rows_dev, dim, hid, emb):
+def finish(got, base, base_in, tail, tails_in, total, layers, rows_dev, dim, hid, emb):
     f32 = jnp.float32
     shards, over = got.shape[0], TAIL
-    wide = base.shape[1]
     nr, nc = (hid + emb) // BLK, dim // BLK
     half = layers * nc
     hbm = pl.BlockSpec(memory_space=pl.ANY)
@@ -975,16 +1085,17 @@
     return pl.pallas_call(
         finish_kernel,
         grid=(2 * half,),
-        in_specs=[pl.BlockSpec(memory_space=pltpu.SMEM), hbm, hbm, pl.BlockSpec((nr, BLK, BLK), block)],
+        in_specs=[pl.BlockSpec(memory_space=pltpu.SMEM), hbm, hbm, hbm, hbm, pl.BlockSpec((nr, BLK, BLK), block)],
         out_specs=[hbm, pl.BlockSpec((1, hid, BLK), tall), pl.BlockSpec((1, emb, BLK), tall),
                    pl.BlockSpec((1, BLK, hid), flat), pl.BlockSpec((1, BLK, emb), flat)],
         out_shape=[S((layers, rows_dev, emb), f32), S((layers, hid, dim), f32), S((layers, emb, dim), f32),
                    S((layers, dim, hid), f32), S((layers, dim, emb), f32)],
-        scratch_shapes=[pltpu.VMEM((shards, BASE, wide), f32), pltpu.VMEM((layers, shards, over, emb), f32),
-                        pltpu.VMEM((layers, rows_dev, emb), f32), pltpu.SemaphoreType.DMA((3,))],
-        compiler_params=pltpu.CompilerParams(vmem_limit_bytes=66_000_000),
+        scratch_shapes=[pltpu.VMEM((layers, shards, BASE, emb), f32), pltpu.VMEM((layers, shards, over, emb), f32),
+                        pltpu.VMEM((layers, rows_dev, emb), f32), pltpu.SemaphoreType.DMA((5,))],
+        compiler_params=pltpu.CompilerParams(vmem_limit_bytes=VMEM_LIMIT),
         name="finish",
-    )(got, base.reshape(shards, BASE, wide), tail.reshape(layers, shards, over, emb), total)
+    )(got, base.reshape(shards, BASE, emb), base_in, tail.reshape(shards, over, emb),
+      tails_in.reshape(layers - 1, shards, over, emb), total)
 
 
 WORK = (1, 2, 1, 0, 0)
@@ -1089,8 +1200,8 @@
         out_specs=[hbm] * len(keep) + [vm] * n,
         out_shape=[S(s, bf) for s in keep] + [S((rows, emb), bf)] * n,
         scratch_shapes=[V((dim, hid + emb), bf), V((hid, dim), bf)] + [V(s, bf) for s in keep] + sems + steps + steps[:-1],
-        compiler_params=pltpu.CompilerParams(collective_id=1, has_side_effects=True, vmem_limit_bytes=66_000_000),
-        cost_estimate=pl.CostEstimate(flops=10**11, bytes_accessed=10**8, transcendentals=0),
+        compiler_params=pltpu.CompilerParams(collective_id=1, has_side_effects=True, vmem_limit_bytes=VMEM_LIMIT),
+        cost_estimate=COST,
         name="tails",
     )(x_in, w_up, w_down, w_gate, *[t.reshape(cube + (rows, emb)) for t in tails])
 
@@ -1101,11 +1212,11 @@
     served = serve(got, ple_tables, TAIL)
     base = swap(served[0].reshape(shards * BASE, layers * emb))
     u, h, a, m, z, g, *rests = run_tails(x_in, w_up, w_down, w_gate, served[1:])
-    x_out, us, as_, ss, os_, dhs, dzs, _, send_b, send_t = run_model(
+    x_out, us, as_, ss, os_, dhs, dzs, _, base_in, tails_in, send_b, send_t = run_model(
         (x_in, m, h, z, g), base, rests, pick, pick_t, d_out, w_up, w_down, w_gate, w_proj)
     base = swap(send_b)
     total, tail = reduce_grads(u, a, us, as_, ss, os_, dhs, dzs, send_t)
-    table, down, proj, up, gate = finish(got, base, tail, total, layers, rows_dev, w_up.shape[1], w_up.shape[2], emb)
+    table, down, proj, up, gate = finish(got, base, base_in, tail, tails_in, total, layers, rows_dev, w_up.shape[1], w_up.shape[2], emb)
     return x_out, table, up, down, gate, proj
 
 
@@ -1139,9 +1250,9 @@
         grad_send = jnp.zeros((shards * cap_rows, d_rows.shape[1]), jnp.float32).at[dest_slot].set(d_rows)
         grad_recv = swap(grad_send)
         tables_by_layer[layer_idx] = jax.ops.segment_sum(grad_recv, req_recv, num_segments=rows_dev)
-    u, a, s, o, dh, dz = ([k[i] for k in kept] for i in range(6))
-    total = reduce_grads(u[0], a[0], jnp.stack(u[1:]), jnp.stack(a[1:]), jnp.stack(s), jnp.stack(o), jnp.stack(dh), jnp.stack(dz), jnp.zeros((TAIL, dz[0].shape[1] * layers), jnp.float32))[0]
-    dim, hid, emb = w_up.shape[1], w_up.shape[2], w_gate.shape[2]
+    u, a, s, o, dh, dz = zip(*kept)
+    total = reduce_grads(u[0], a[0], jnp.stack(u[1:]), jnp.stack(a[1:]), jnp.stack(s), jnp.stack(o), jnp.stack(dh), jnp.stack(dz), jnp.zeros((TAIL, dz[0].shape[1]), jnp.float32))[0]
+    (_, dim, hid), (_, _, emb) = w_up.shape, w_gate.shape
     nr, nc = (hid + emb) // BLK, dim // BLK
     total = total.reshape(layers, 2, nr * nc, BLK, BLK)
     tall = total[:, 0].reshape(layers, nc, nr, BLK, BLK).transpose(0, 2, 3, 1, 4).reshape(layers, hid + emb, dim)
@@ -1157,7 +1268,12 @@
         tables = rest[2]
         pick, pick_t, got = spread(tok_ids, shards, tables.shape[1])
         fits = jnp.max(got[:, 3]) <= TAIL
-        return lax.cond(fits, lambda: fast_step(got, pick, pick_t, *rest), lambda: tuple(padded_step(shards, tok_ids, *rest)))
+        outs = fast_step(got, pick, pick_t, *rest)
+
+        def again(_):
+            return jnp.bool_(True), padded_step(shards, tok_ids, *rest)
+
+        return lax.while_loop(lambda state: jnp.logical_not(state[0]), again, (fits, outs))[1]
 
     return jax.shard_map(
         device_step,

time: 963 us -> 892 us (0.926)
  Pallas kernels: 909 us -> 845 us
    pallas_call x1, Pallas kernels: 638 us -> 555 us  [reduce_grads(): pl.pallas_call(functools.partial(reduce_kernel, (n_layers, per, n)), out_...]
    pallas_call x1, Pallas kernels: 121 us -> 142 us  [run_model(): pl.pallas_call(model_kernel, in_specs=[hbm] * 3 + [vm] * 6 + [hbm] + [vm]...]
  transfers between devices with their start and end apart: 3 -> 3, of which waited for: 1 -> 1; matrix products, arithmetic and copies ran while one was open for 0% -> 0% of each run, Pallas kernels for 73% -> 70%
where the time goes in v2:
time: 892 us; the launch traced here: 887 us
  Pallas kernels  845 us (95%)
  starting transfers between devices  14.3 us (2%)
  other arithmetic  11.4 us (1%)
    pallas_call x1, Pallas kernels, reduce_grads(): pl.pallas_call(functools.partial(reduce_kernel, (n_layers, per, n)), out_...  555 us
    pallas_call x1, Pallas kernels, run_model(): pl.pallas_call(model_kernel, in_specs=[hbm] * 3 + [vm] * 6 + [hbm] + [vm]...  142 us
    pallas_call x1, Pallas kernels, finish(): pl.pallas_call(finish_kernel, grid=(2 * half,), in_specs=[pl.BlockSpec(me...  69.6 us
    pallas_call x1, Pallas kernels, run_tails(): pl.pallas_call(tails_kernel, in_specs=[vm] + [hbm] * 3 + [vm] * n, out_sp...  62.6 us
  transfers between devices with their start and end apart: 3, of which 1 were waited for; matrix products, arithmetic and copies ran while one was open for 0% of the time, Pallas kernels for 70%

profile of v2, /device:TPU:0, one launch (start us, length us, event | category | flops | bytes accessed | tf_op | source)
XLA Modules:
  0.0 886.5 jit_solution(3712990490159323662)
XLA Ops:
  0.6 1.9 convert_reduce_fusion.1
  2.5 0.7 add_select_fusion.3
  3.2 0.1 select_reduce_fusion
  3.4 0.6 fusion.222
  4.6 0.1 select_reduce_fusion.2
  4.7 0.1 select_reduce_fusion.1
  4.8 0.5 fusion.208
  5.4 0.7 subtract_multiply_fusion
  6.1 1.3 fusion.204
  7.4 0.9 fusion.202
  8.3 2.4 fusion.201.refs_10_
  10.8 0.1 pad.20.clone
  10.9 0.1 pad.22.clone
  10.9 0.1 slice.104
  11.0 0.7 pad.28.clone
  11.7 0.1 maximum_convert_fusion
  11.8 0.1 copy.97
  11.9 0.7 all_to_all.74
  12.6 7.3 all-to-all-start.7
  19.9 1.9 fusion.203.refs_9_
  21.8 5.5 all-to-all-done.7
  27.2 0.6 copy.114
  27.8 15.1 %serve_rows.1 = (bf16[32,32,768]{2,1,0:T(8,128)(2,1)}, bf16[32,128,256]{2,1,0:T(8,128)(2,1)}, bf16[32,128,256]{2,1,0:T(8,128)(2,1)}, bf16[32,128,256]{2,1,0:T(8,128)(2,1)}) custom-call(s32[32,288]{1,0:T(8,128)} %bitcast.246, bf16[3,4748,256]{2,1,0:T(8,128)(2,1)} %tables.1), custom_call_target="tpu_custom_call" | custom-call | tf_op jit(solution)/shard_map/serve_rows/pallas_call | solution.py:957
  42.9 3.6 all-to-all-start.8
  46.5 62.6 %tails.1 = (bf16[1024,1024]{1,0:T(8,128)(2,1)}, bf16[1024,3072]{1,0:T(8,128)(2,1)}, bf16[1024,3072]{1,0:T(8,128)(2,1)}, bf16[1024,1024]{1,0:T(8,128)(2,1)}, bf16...) custom-call(bf16[1024,1024]{1,0:T(8,128)(2,1)} %refs_0_.3, ...), custom_call_target="tpu_custom_call" | custom-call | flops 99999997952 | bytes 100000000 | tf_op jit(solution)/shard_map/tails/pallas_call | solution.py:1197
  109.1 1.4 slice_reduce_fusion
  111.2 142.4 %model.1 = (bf16[1024,1024]{1,0:T(8,128)(2,1)}, bf16[2,1024,1024]{2,1,0:T(8,128)(2,1)}, bf16[2,1024,3072]{2,1,0:T(8,128)(2,1)}, bf16[3,1024,256]{2,1,0:T(8,128)(...) custom-call(bf16[1024,1024]{1,0:T(8,128)(2,1)} %refs_0_.3, ...), custom_call_target="tpu_custom_call" | custom-call | tf_op jit(solution)/shard_map/model/pallas_call | solution.py:824
  253.6 3.4 all-to-all-start.9
  257.0 555.4 %reduce_grads.3 = (f32[312,256,256]{2,1,0:T(8,128)}, f32[2,2,2,2,2,128,256]{6,5,4,3,2,1,0:T(8,128)}) custom-call(bf16[1024,1024]{1,0:T(8,128)(2,1)} %get-tuple-element.129.refs_0_, bf16[1024,3072]{1,0:T(8,128)(2,1)} %get-tuple-element.130.refs_1_, bf16[2,1024,1024]{2,1,0:T(8,128)(2,1)} %get-tuple-element.131.refs_2_, ...), custom_call_target="tpu_custom_call" | custom-call | flops 99999997952 | bytes 100000000 | tf_op jit(solution)/shard_map/reduce_grads/pallas_call | solution.py:432
  812.4 69.6 %finish.1 = (f32[3,4748,256]{2,1,0:T(8,128)}, f32[3,3072,1024]{2,1,0:T(8,128)}, f32[3,256,1024]{2,1,0:T(8,128)}, f32[3,1024,3072]{2,1,0:T(8,128)}, f32[3,1024,256]{2,1,0:T(8,128)}) custom-call(s32[32,288]{1,0:T(8,128)} %bitcast.248, f32[32,32,256]{2,1,0:T(8,128)} %all-to-all-done.9.base, f32[2,32,32,256]{3,2,1,0:T(8,128)} %get-tuple-element.128.base_in, ...), custom_call_target="tpu_custom_call" | custom-call | tf_op jit(solution)/shard_map/finish/pallas_call | solution.py:1085
  882.0 1.2 while.19
  883.2 3.1 copy.139
  (13 shorter events, 0.1 us)
Async XLA Ops:
  12.6 14.7 %all-to-all-start.7 = ((s32[32,1,288]{2,1,0:T(1,128)}), s32[32,1,288]{2,1,0:T(1,128)S(1)}, u32[]{:S(2)}, u32[]{:S(2)}) async-start(s32[32,1,288]{2,1,0:T(1,128)} %all_to_all.74), calls=%async_computation.7 | async-start | bytes 98304 | tf_op jit(solution)/shard_map/all_to_all | solution.py:91
  42.9 68.3 %all-to-all-start.8 = ((bf16[32,32,768]{2,1,0:T(8,128)(2,1)}), bf16[32,32,768]{2,1,0:T(8,128)(2,1)}, u32[]{:S(2)}, u32[]{:S(2)}) async-start(bf16[32,32,768]{2,1,0:T(8,128)(2,1)} %get-tuple-element.122), calls=%async_computation.8 | async-start | bytes 3145728 | tf_op jit(solution)/shard_map/all_to_all | solution.py:91
  253.6 558.8 %all-to-all-start.9 = ((f32[32,32,256]{2,1,0:T(8,128)}), f32[32,32,256]{2,1,0:T(8,128)}, u32[]{:S(2)}, u32[]{:S(2)}) async-start(f32[32,32,256]{2,1,0:T(8,128)} %bitcast.245), calls=%async_computation.9 | async-start | bytes 2097152 | tf_op jit(solution)/shard_map/all_to_all | solution.py:91
  812.4 69.6 %copy-start.29 = (s32[1024]{0:T(1024)S(1)}, s32[1024]{0:T(1024)}, u32[]{:S(2)}) copy-start(s32[1024]{0:T(1024)} %param.14) | copy-start | bytes 12292
